TPU v7x, 768 devices: a whole 4x8x12 slice. The times are simulated.
768 devices in a mesh: replica: 8 (over y_lo, core), shard: 96 (over z, y_hi, x).
Axes of the slice: x: 4, y: 8 (y_hi: 2, y_lo: 4; y = y_hi * 4 + y_lo), z: 12, core: 2. Of those that a mesh axis runs over, the one named last changes fastest.
Arguments:
- anchor: float32 [4608, 8192], P('shard'), may hold values from -6 to 6
- replica_rows: bfloat16 [8, 4608, 8192], P('replica', 'shard'), may hold values from -6 to 6
- outer_velocity: float32 [4608, 8192], P('shard', 'replica'), may hold values from -6 to 6
- features: bfloat16 [8, 4608, 3072], P('replica', 'shard'), may hold values from -6 to 6
- cotangent: bfloat16 [8, 3072, 1024], P('replica', 'shard'), may hold values from -0.109375 to 0.109375
- inner_weight: float32 [8, 4608, 1024], P('replica', 'shard'), may hold values from -6 to 6
- first_moment: float32 [8, 4608, 1024], P('replica', 'shard'), may hold values from -6 to 6
- second_moment: float32 [8, 4608, 1024], P('replica', 'shard'), may hold values from 0.5 to 2
Outputs:
- new_anchor: float32 [4608, 8192], P('shard')
- merged_rows: bfloat16 [8, 4608, 8192], P('replica', 'shard')
- new_velocity: float32 [4608, 8192], P('shard', 'replica')
- new_weight: float32 [8, 4608, 1024], P('replica', 'shard')
- new_first: float32 [8, 4608, 1024], P('replica', 'shard')
- new_second: float32 [8, 4608, 1024], P('replica', 'shard')
All inputs are finite; a program needn't handle non-finite values.
Results may differ from a plain program's by a relative error of at most 0.0035.
Values may be sent and summed in bfloat16 or wider, within the bound.
No kernel may reach another device: no remote copies, remote signals or barrier semaphores. Data moves between devices by JAX's collectives and lax.ppermute only.
A program may use at most 64 MiB of HBM per device.

v0:
```python
import jax
import jax.numpy as jnp
from jax import lax
from jax.sharding import Mesh
from jax.sharding import PartitionSpec as P

SHARD = ("shard_0", "shard_1", "shard_2")


momentum_keep = 0.9
outer_rate = 0.7
blend_keep = 0.5
inner_rate = 0.01
decay_first = 0.9
decay_second = 0.95
weight_decay = 0.1
epsilon = 1e-08
first_fix = 1.0 - 0.9**10
second_fix = 1.0 - 0.95**10


def split_up(x, dim, length):
    before, after = (x.shape[:dim], x.shape[dim + 1 :])
    return jnp.moveaxis(x.reshape(*before, length, -1, *after), dim, 0)


def sent_and_summed(x, axis, dim):
    length = lax.axis_size(axis)
    pieces = lax.all_to_all(split_up(x, dim, length), axis, 0, 0, tiled=True)
    return jnp.sum(pieces, axis=0)


def laid_out(pieces, dim):
    dims = list(pieces.shape[1:])
    dims[dim] *= pieces.shape[0]
    return jnp.moveaxis(pieces, 0, dim).reshape(dims)


def sent_to_all(x, axis):
    copies = jnp.broadcast_to(x, (lax.axis_size(axis), *x.shape))
    return lax.all_to_all(copies, axis, split_axis=0, concat_axis=0, tiled=True)


def collect(x, axis, dim):
    return laid_out(sent_to_all(x, axis), dim)


def stacked_from(x, axes, turns):
    pieces = x[None]
    for k in turns:
        pieces = lax.all_gather(pieces, axes[k], axis=0, tiled=True)
    current = [lax.axis_size(axes[k]) for k in reversed(turns)]
    pieces = pieces.reshape(*current, *x.shape)
    turned = sorted(range(len(turns)), key=lambda place: turns[len(turns) - 1 - place])
    return pieces.transpose(*turned, *range(len(turns), pieces.ndim)).reshape(-1, *x.shape)


def gathered_by_axis(x, axes, turns, dim):
    return laid_out(stacked_from(x, axes, turns), dim)


def outer_sync(anchor, replica_rows, outer_velocity):
    replicas = lax.axis_size("replica")
    own_rows = replica_rows[0].astype(jnp.float32)
    slice_width = outer_velocity.shape[1]
    offset = lax.axis_index("replica") * slice_width
    drift = anchor - own_rows
    shared = sent_and_summed(drift, "replica", 1)
    outer_grad = shared / replicas
    new_velocity = momentum_keep * outer_velocity + outer_grad
    anchor_part = lax.dynamic_slice_in_dim(anchor, offset, slice_width, 1)
    anchor_part = anchor_part - outer_rate * (outer_grad + momentum_keep * new_velocity)
    new_anchor = collect(anchor_part, "replica", 1)
    merged_rows = (blend_keep * own_rows + (1.0 - blend_keep) * new_anchor).astype(jnp.bfloat16)
    return (new_anchor, merged_rows[None], new_velocity)


def inner_update(features, cotangent, inner_weight, first_moment, second_moment):
    feature_rows = features[0]
    gradient = jnp.dot(
        feature_rows,
        gathered_by_axis(cotangent, SHARD, (1, 0, 2), 1)[0],
        preferred_element_type=jnp.float32,
    )[None]
    new_first = decay_first * first_moment + (1.0 - decay_first) * gradient
    new_second = decay_second * second_moment + (1.0 - decay_second) * gradient * gradient
    stepped = new_first / first_fix / (jnp.sqrt(new_second / second_fix) + epsilon)
    new_weight = inner_weight - inner_rate * (stepped + weight_decay * inner_weight)
    return (new_weight, new_first, new_second)


def local(
    anchor,
    replica_rows,
    outer_velocity,
    features,
    cotangent,
    inner_weight,
    first_moment,
    second_moment,
):
    new_weight, new_first, new_second = inner_update(
        features, cotangent, inner_weight, first_moment, second_moment
    )
    new_anchor, merged_rows, new_velocity = outer_sync(anchor, replica_rows, outer_velocity)
    return (new_anchor, merged_rows, new_velocity, new_weight, new_first, new_second)


def solution(mesh):
    split = Mesh(
        mesh.devices.reshape(mesh.shape["replica"], 12, 2, 4),
        ("replica", "shard_0", "shard_1", "shard_2"),
    )
    return jax.shard_map(
        local,
        mesh=split,
        in_specs=(
            P(SHARD, None),
            P("replica", SHARD, None),
            P(SHARD, "replica"),
            P("replica", SHARD, None),
            P("replica", SHARD, None),
            P("replica", SHARD, None),
            P("replica", SHARD, None),
            P("replica", SHARD, None),
        ),
        out_specs=(
            P(SHARD, None),
            P("replica", SHARD, None),
            P(SHARD, "replica"),
            P("replica", SHARD, None),
            P("replica", SHARD, None),
            P("replica", SHARD, None),
        ),
        check_vma=False,
    )
```

profile of v0, /device:TPU:1, one launch (start us, length us, event | category | flops | bytes accessed | tf_op | source)
XLA Modules:
  0.0 192.3 jit_solution(6038950936327479635)
XLA Ops:
  7.2 0.0 copy-start
  7.2 0.0 copy-start.1
  7.2 0.0 all-gather.6.cloned.1.call-start
  7.2 10.7 %all-gather = bf16[2,32,1024]{2,1,0:T(8,128)(2,1)} all-gather(bf16[1,32,1024]{2,1,0:T(8,128)(2,1)} %param.12), channel_id=2, replica_groups=mesh['replica'=8,'shard_0'=12,'shard_1'=2,'shard_2'=4] {'shard_1'}, dimensions={0}, use_global_device_ids=true | all-gather | bytes 196608 | tf_op jit(solution)/shard_map/all_gather | solution.py:51
  17.9 0.0 all-gather.6.cloned.1.call-update
  18.0 0.0 all-gather.8.cloned.1.call-start
  18.0 60.2 %all-gather.6.cloned.1.call-done = bf16[24,32,1024]{2,1,0:T(8,128)(2,1)} async-done(((bf16[2,32,1024]{2,1,0:T(8,128)(2,1)}), bf16[24,32,1024]{2,1,0:T(8,128)(2,1)}) %all-gather.6.cloned.1.call-update) | async-done | bytes 1572880 | tf_op jit(solution)/shard_map/all_gather | solution.py:51
  78.2 0.0 all-gather.8.cloned.1.call-update
  78.2 0.0 copy-done.1
  78.2 1.5 fusion
  79.8 0.9 copy.21
  80.7 2.1 %copy.16 = f32[8,48,1024]{2,1,0:T(8,128)} copy(f32[8,48,1024]{2,0,1:T(8,128)S(1)} %bitcast.33) | data formatting | bytes 3145728 | tf_op jit(solution)/shard_map/transpose | solution.py:24
  82.7 11.9 %all-to-all-start = ((f32[8,48,1024]{2,1,0:T(8,128)}), f32[8,48,1024]{2,1,0:T(8,128)S(1)}, u32[]{:S(2)}, u32[]{:S(2)}) async-start(f32[8,48,1024]{2,1,0:T(8,128)} %copy.16), calls=%async_computation | async-start | bytes 3145728 | tf_op jit(solution)/shard_map/all_to_all | solution.py:29
  94.6 0.0 copy-start.3
  94.6 36.9 %all-to-all-done = f32[8,48,1024]{2,1,0:T(8,128)S(1)} async-done(((f32[8,48,1024]{2,1,0:T(8,128)}), f32[8,48,1024]{2,1,0:T(8,128)S(1)}, u32[]{:S(2)}, u32[]{:S(2)}) %all-to-all-start) | async-done | bytes 1572896 | tf_op jit(solution)/shard_map/all_to_all | solution.py:29
  131.6 0.1 reduce_sum.9
  131.7 0.0 copy-done.3
  131.7 1.7 multiply_subtract_fusion.1
  133.3 0.2 broadcast_in_dim.8
  133.5 40.1 %all_to_all.10 = f32[8,48,1024]{2,1,0:T(8,128)S(1)} all-to-all(f32[8,48,1024]{2,1,0:T(8,128)S(1)} %broadcast_in_dim.8), channel_id=1, replica_groups=mesh['replica'=8,'shard_0'=12,'shard_1'=2,'shard_2'=4] {'replica'}, dimensions={0} | all-to-all | bytes 3145728 | tf_op jit(solution)/shard_map/all_to_all | solution.py:41
  173.6 2.1 %copy.17 = f32[48,8,1024]{2,1,0:T(8,128)} copy(f32[48,8,1024]{2,0,1:T(8,128)S(1)} %bitcast.30) | data formatting | bytes 3145728 | tf_op jit(solution)/shard_map/transpose | solution.py:36
  175.6 1.6 reshape.31
  177.2 0.0 copy-start.2
  177.2 1.2 copy.20
  178.4 0.1 copy-done.2
  178.6 1.1 fusion.2
  179.7 3.6 %copy.19 = bf16[12,2,4,1,32,1024]{5,4,2,1,0,3:T(8,128)(2,1)S(1)} copy(bf16[12,2,4,1,32,1024]{5,4,1,0,2,3:T(8,128)(2,1)} %bitcast.32) | data formatting | bytes 12582912 | tf_op jit(solution)/shard_map/transpose | solution.py:55
  183.2 0.0 copy-done
  183.2 0.0 copy-done.4
  183.3 0.0 copy-done.5
  183.3 0.0 copy-done.6
  183.3 2.2 %multiply_subtract_fusion = (f32[1,48,1024]{2,1,0:T(8,128)}, f32[1,48,1024]{2,1,0:T(8,128)}, f32[1,48,1024]{2,1,0:T(8,128)}) fusion(f32[1,48,1024]{2,1,0:T(8,128)S(1)} %copy-done.4, f32[1,48,1024]{2,1,0:T(8,128)S(1)} %copy-done.5, f32[1,48,1024]{2,1,0:T(8,128)S(1)} %copy-done.6, bf16[3072,1024]{1,0:T(8,128)(2,1)S(1)} %bitcast.29, ...), kind=kOutput, calls=%fused_computation.11 | convolution fusion | flops 302727168 | bytes 7766016 | tf_op jit(solution)/shard_map/dot_general | solution.py:80
  (4 shorter events, 0.0 us)
Async XLA Ops:
  7.2 176.1 %copy-start = (bf16[1,48,3072]{2,1,0:T(8,128)(2,1)S(1)}, bf16[1,48,3072]{2,1,0:T(8,128)(2,1)}, u32[]{:S(2)}) copy-start(bf16[1,48,3072]{2,1,0:T(8,128)(2,1)} %param.11) | copy-start | bytes 884740
  7.2 71.0 %copy-start.1 = (bf16[1,48,8192]{2,1,0:T(8,128)(2,1)S(1)}, bf16[1,48,8192]{2,1,0:T(8,128)(2,1)}, u32[]{:S(2)}) copy-start(bf16[1,48,8192]{2,1,0:T(8,128)(2,1)} %param.9) | copy-start | bytes 2359300
  7.2 71.0 %all-gather.6.cloned.1.call-start = ((), (), s32[]{:S(2)}) async-start(), calls=%async_computation.2 | async-start | bytes 1703936 | tf_op jit(solution)/shard_map/all_gather | solution.py:51
  18.0 161.7 %all-gather.8.cloned.1.call-start = ((), (), s32[]{:S(2)}) async-start(), calls=%async_computation.3 | async-start | bytes 7864320 | tf_op jit(solution)/shard_map/all_gather | solution.py:51
  82.7 48.8 %all-to-all-start = ((f32[8,48,1024]{2,1,0:T(8,128)}), f32[8,48,1024]{2,1,0:T(8,128)S(1)}, u32[]{:S(2)}, u32[]{:S(2)}) async-start(f32[8,48,1024]{2,1,0:T(8,128)} %copy.16), calls=%async_computation | async-start | bytes 3145728 | tf_op jit(solution)/shard_map/all_to_all | solution.py:29
  94.6 37.0 %copy-start.3 = (f32[48,1024]{1,0:T(8,128)S(1)}, f32[48,1024]{1,0:T(8,128)}, u32[]{:S(2)}) copy-start(f32[48,1024]{1,0:T(8,128)} %param.10) | copy-start | bytes 589828
  177.2 1.4 copy-start.2
  179.7 3.6 %copy-start.4 = (f32[1,48,1024]{2,1,0:T(8,128)S(1)}, f32[1,48,1024]{2,1,0:T(8,128)}, u32[]{:S(2)}) copy-start(f32[1,48,1024]{2,1,0:T(8,128)} %param.13) | copy-start | bytes 589828
  179.7 3.6 %copy-start.5 = (f32[1,48,1024]{2,1,0:T(8,128)S(1)}, f32[1,48,1024]{2,1,0:T(8,128)}, u32[]{:S(2)}) copy-start(f32[1,48,1024]{2,1,0:T(8,128)} %param.14) | copy-start | bytes 589828
  179.7 3.6 %copy-start.6 = (f32[1,48,1024]{2,1,0:T(8,128)S(1)}, f32[1,48,1024]{2,1,0:T(8,128)}, u32[]{:S(2)}) copy-start(f32[1,48,1024]{2,1,0:T(8,128)} %param.15) | copy-start | bytes 589828
Sparse Core Ops, SparseCore 0:
  18.1 60.0 all-gather.5
  80.6 77.0 all-gather.7
where the time goes:
time: 193 us; the launch traced here: 192 us
  waiting for transfers between devices  97.2 us (50%)
  blocking collectives  50.7 us (26%)
  between operations  14.2 us (7%)
  starting transfers between devices  12 us (6%)
  local copies, waits for them, and re-layouts  11.7 us (6%)
  other arithmetic  4.38 us (2%)
  matrix products  2.16 us (1%)
    all_gather x2, waiting for transfers between devices, stacked_from(): pieces = lax.all_gather(pieces, axes[k], axis=0, tiled=True)  60.2 us
    all_to_all x1, blocking collectives, sent_to_all(): return lax.all_to_all(copies, axis, split_axis=0, concat_axis=0, tiled=True)  40.1 us
    all_to_all x1, waiting for transfers between devices, sent_and_summed(): pieces = lax.all_to_all(split_up(x, dim, length), axis, 0, 0, tiled=True)  36.9 us
    all_to_all x1, starting transfers between devices, sent_and_summed(): pieces = lax.all_to_all(split_up(x, dim, length), axis, 0, 0, tiled=True)  11.9 us
    all_gather x1, blocking collectives, stacked_from(): pieces = lax.all_gather(pieces, axes[k], axis=0, tiled=True)  10.7 us
  transfers between devices with their start and end apart: 3, of which 2 were waited for; matrix products, arithmetic and copies ran while one was open for 6% of the time, Pallas kernels for 0%

commit v1 on v0

v1 whole, which is shorter than its diff:
```python
import jax
import jax.numpy as jnp
from jax import lax
from jax.experimental import pallas as pl
from jax.experimental.pallas import tpu as pltpu
from jax.sharding import Mesh
from jax.sharding import PartitionSpec as P

REPLICA = ("y_near", "core")
SHARD = ("z_pair", "z_bit", "y_far", "x")
GROUP = ("z_bit", "x")


momentum_keep = 0.9
outer_rate = 0.7
blend_keep = 0.5
inner_rate = 0.01
decay_first = 0.9
decay_second = 0.95
weight_decay = 0.1
epsilon = 1e-08
first_fix = 1.0 - 0.9**10
second_fix = 1.0 - 0.95**10

LANES = 128


def pack_kernel(features_ref, out_ref):
    rows, tokens = features_ref.shape
    piece = LANES // 4
    lane = lax.broadcasted_iota(jnp.int32, (rows, LANES), 1)
    for block in range(tokens // (8 * LANES)):
        for bit in range(2):
            tiles = []
            for place in range(4):
                column = (block * 2 + place // 2) * 4 + bit * 2 + place % 2
                tiles.append(features_ref[:, column * LANES : (column + 1) * LANES].astype(jnp.float32))
            for x in range(4):
                packed = jnp.zeros((rows, LANES), jnp.float32)
                for place in range(4):
                    shift = (place - x) * piece % LANES
                    turned = pltpu.roll(tiles[place], shift, 1) if shift else tiles[place]
                    packed = jnp.where(lane // piece == place, turned, packed)
                out_ref[bit * 4 + x, :, block * LANES : (block + 1) * LANES] = packed.astype(jnp.bfloat16)


def packed_by_token(features):
    rows, tokens = features.shape
    return pl.pallas_call(
        pack_kernel,
        out_shape=jax.ShapeDtypeStruct((8, rows, tokens // 8), jnp.bfloat16),
        name="pack",
    )(features)


def exchange(x, axes):
    return lax.all_to_all(x, axes, 0, 0, tiled=True)


def local(
    anchor,
    replica_rows,
    outer_velocity,
    features,
    cotangent,
    inner_weight,
    first_moment,
    second_moment,
):
    replicas = lax.axis_size(REPLICA)
    rows = replica_rows[0]
    height, width = rows.shape
    part = outer_velocity.shape[1]

    packed = packed_by_token(features[0])
    other = lax.ppermute(cotangent[0], "y_far", [(0, 1), (1, 0)])
    own_tokens = exchange(packed, GROUP)
    own_tokens = own_tokens.reshape(-1, own_tokens.shape[-1])

    first = lax.axis_index("y_far") == 0
    both = jnp.where(
        first,
        jnp.concatenate([cotangent[0], other]),
        jnp.concatenate([other, cotangent[0]]),
    )
    pieces = jnp.moveaxis(rows.reshape(height, replicas, part), 1, 0)
    pieces, own_tokens, both = lax.optimization_barrier((pieces, own_tokens, both))
    pieces = exchange(pieces, REPLICA)

    own_cotangent = lax.all_gather(both, "z_pair", axis=0, tiled=True)

    partial = jnp.dot(own_tokens, own_cotangent, preferred_element_type=jnp.float32)
    partial = partial.astype(jnp.bfloat16).reshape(-1, height, partial.shape[1])
    partial, pieces = lax.optimization_barrier((partial, pieces))
    parts = exchange(partial, GROUP)

    offset = lax.axis_index(REPLICA) * part
    anchor_part = lax.dynamic_slice_in_dim(anchor, offset, part, 1)
    outer_grad = jnp.sum(anchor_part[None] - pieces.astype(jnp.float32), axis=0) / replicas
    new_velocity = momentum_keep * outer_velocity + outer_grad
    moved = anchor_part - outer_rate * (outer_grad + momentum_keep * new_velocity)
    moved = lax.all_gather(moved.astype(jnp.bfloat16), REPLICA, axis=0)
    new_anchor = jnp.moveaxis(moved, 0, 1).reshape(height, width).astype(jnp.float32)
    merged_rows = (blend_keep * rows.astype(jnp.float32) + (1.0 - blend_keep) * new_anchor).astype(jnp.bfloat16)

    gradient = jnp.sum(parts.astype(jnp.float32), axis=0)[None]
    new_first = decay_first * first_moment + (1.0 - decay_first) * gradient
    new_second = decay_second * second_moment + (1.0 - decay_second) * gradient * gradient
    stepped = new_first / first_fix / (jnp.sqrt(new_second / second_fix) + epsilon)
    new_weight = inner_weight - inner_rate * (stepped + weight_decay * inner_weight)
    return (new_anchor, merged_rows[None], new_velocity, new_weight, new_first, new_second)


def solution(mesh):
    split = Mesh(
        mesh.devices.reshape(4, 2, 6, 2, 2, 4),
        REPLICA + SHARD,
    )
    return jax.shard_map(
        local,
        mesh=split,
        in_specs=(
            P(SHARD, None),
            P(REPLICA, SHARD, None),
            P(SHARD, REPLICA),
            P(REPLICA, SHARD, None),
            P(REPLICA, SHARD, None),
            P(REPLICA, SHARD, None),
            P(REPLICA, SHARD, None),
            P(REPLICA, SHARD, None),
        ),
        out_specs=(
            P(SHARD, None),
            P(REPLICA, SHARD, None),
            P(SHARD, REPLICA),
            P(REPLICA, SHARD, None),
            P(REPLICA, SHARD, None),
            P(REPLICA, SHARD, None),
        ),
        check_vma=False,
    )
```

time: 193 us -> 97.3 us (0.50)
  waiting for transfers between devices: 97.2 us -> 1.46 us
  starting transfers between devices: 12 us -> 32.4 us
  between operations: 14.2 us -> 0.77 us
  blocking collectives: 50.7 us -> 44.3 us
  local copies, waits for them, and re-layouts: 11.7 us -> 6.73 us
  other arithmetic: 4.38 us -> 6.46 us
  Pallas kernels: 0 us -> 2.05 us
    all_gather x2 -> x0, waiting for transfers between devices: 60.2 us -> none  [stacked_from(): pieces = lax.all_gather(pieces, axes[k], axis=0, tiled=True)]
    all_to_all x1 -> x0, blocking collectives: 40.1 us -> none  [sent_to_all(): return lax.all_to_all(copies, axis, split_axis=0, concat_axis=0, tiled=True)]
    all_to_all x1 -> x3, waiting for transfers between devices: 36.9 us -> 0.01 us  [exchange(): return lax.all_to_all(x, axes, 0, 0, tiled=True)]
    all_gather x1 -> x2, blocking collectives: 10.7 us -> 44.3 us  [the longest x1 25.8 us: local(): own_cotangent = lax.all_gather(both, 'z_pair', axis=0, tiled=True)]
    all_to_all x1 -> x3, starting transfers between devices: 11.9 us -> 25 us  [exchange(): return lax.all_to_all(x, axes, 0, 0, tiled=True)]
    transpose x3 -> x0, local copies, waits for them, and re-layouts: 7.67 us -> none  [the longest x1 3.56 us: stacked_from(): pieces.transpose(*turned, *range(len(turns), pieces.ndim))]
    ppermute x0 -> x1, starting transfers between devices: none -> 7.44 us  [local(): other = lax.ppermute(cotangent[0], 'y_far', [(0, 1), (1, 0)])]
    convert_element_type x0 -> x3, local copies, waits for them, and re-layouts: none -> 4 us  [local(): jnp.moveaxis(moved, 0, 1).reshape(height, width).astype(jnp.float32)]
  transfers between devices with their start and end apart: 3 -> 4, of which waited for: 2 -> 1; matrix products, arithmetic and copies ran while one was open for 6% -> 12% of each run, Pallas kernels for 0% -> 0%
where the time goes in v1:
time: 97.3 us; the launch traced here: 95.6 us
  blocking collectives  44.3 us (46%)
  starting transfers between devices  32.4 us (33%)
  local copies, waits for them, and re-layouts  6.73 us (7%)
  other arithmetic  6.46 us (7%)
  Pallas kernels  2.05 us (2%)
  waiting for transfers between devices  1.46 us (2%)
  matrix products  1.46 us (2%)
    all_gather x1, blocking collectives, local(): own_cotangent = lax.all_gather(both, 'z_pair', axis=0, tiled=True)  25.8 us
    all_to_all x3, starting transfers between devices, exchange(): return lax.all_to_all(x, axes, 0, 0, tiled=True)  25 us
    all_gather x1, blocking collectives, local(): moved = lax.all_gather(moved.astype(jnp.bfloat16), REPLICA, axis=0)  18.5 us
    ppermute x1, starting transfers between devices, local(): other = lax.ppermute(cotangent[0], 'y_far', [(0, 1), (1, 0)])  7.44 us
    convert_element_type x3, local copies, waits for them, and re-layouts, local(): jnp.moveaxis(moved, 0, 1).reshape(height, width).astype(jnp.float32)  4 us
    pallas_call x1, Pallas kernels, packed_by_token(): pl.pallas_call(pack_kernel, out_shape=jax.ShapeDtypeStruct((8, rows, toke...  2.05 us
  transfers between devices with their start and end apart: 4, of which 1 were waited for; matrix products, arithmetic and copies ran while one was open for 12% of the time, Pallas kernels for 0%

profile of v1, /device:TPU:1, one launch (start us, length us, event | category | flops | bytes accessed | tf_op | source)
XLA Modules:
  0.0 95.6 jit_solution(1070574123527291960)
XLA Ops:
  0.6 0.0 copy-start.6
  0.6 0.0 copy-start
  0.7 2.1 %pack.1 = bf16[8,48,384]{2,1,0:T(8,128)(2,1)} custom-call(bf16[48,3072]{1,0:T(8,128)(2,1)} %bitcast.30), custom_call_target="tpu_custom_call" | custom-call | tf_op jit(solution)/shard_map/pack/pallas_call | solution.py:49
  2.7 6.6 %all-to-all-start = ((bf16[8,48,384]{2,1,0:T(8,128)(2,1)}), bf16[8,48,384]{2,1,0:T(8,128)(2,1)S(1)}, u32[]{:S(2)}, u32[]{:S(2)}) async-start(bf16[8,48,384]{2,1,0:T(8,128)(2,1)} %pack.1), calls=%async_computation | async-start | bytes 589824 | tf_op jit(solution)/shard_map/all_to_all | solution.py:57
  9.4 7.4 %collective-permute-start = (bf16[32,1024]{1,0:T(8,128)(2,1)}, bf16[32,1024]{1,0:T(8,128)(2,1)S(1)}, u32[]{:S(2)}, u32[]{:S(2)}) collective-permute-start(bf16[32,1024]{1,0:T(8,128)(2,1)} %bitcast.31), channel_id=1, source_target_pairs={{0,4},{4,0},{1,5},{5,1},{2,6},{6,2},{3,7},{7,3},{8,12},{12,8},{9,1... | collective-permute-start | bytes 196616 | tf_op jit(solution)/shard_map/ppermute | solution.py:76
  16.8 0.0 copy-done
  16.8 0.4 copy.22
  17.3 1.5 %collective-permute-done = bf16[32,1024]{1,0:T(8,128)(2,1)S(1)} collective-permute-done((bf16[32,1024]{1,0:T(8,128)(2,1)}, bf16[32,1024]{1,0:T(8,128)(2,1)S(1)}, u32[]{:S(2)}, u32[]{:S(2)}) %collective-permute-start) | collective-permute-done | bytes 65568 | tf_op jit(solution)/shard_map/ppermute | solution.py:76
  18.7 0.0 copy-done.6
  18.8 0.0 all-to-all-done
  18.8 1.3 %copy.18 = bf16[8,48,1024]{2,1,0:T(8,128)(2,1)} copy(bf16[8,48,1024]{2,0,1:T(8,128)(2,1)S(1)} %bitcast.25) | data formatting | bytes 1572864 | tf_op jit(solution)/shard_map/optimization_barrier | solution.py:87
  20.1 11.6 %all-to-all-start.1 = ((bf16[8,48,1024]{2,1,0:T(8,128)(2,1)}), bf16[8,48,1024]{2,1,0:T(8,128)(2,1)S(1)}, u32[]{:S(2)}, u32[]{:S(2)}) async-start(bf16[8,48,1024]{2,1,0:T(8,128)(2,1)} %copy.18), calls=%async_computation.1 | async-start | bytes 1572864 | tf_op jit(solution)/shard_map/all_to_all | solution.py:57
  31.7 0.9 constant_dynamic-slice_fusion
  32.6 25.8 %all_gather.9 = bf16[384,1024]{1,0:T(8,128)(2,1)S(1)} all-gather(bf16[64,1024]{1,0:T(8,128)(2,1)S(1)} %maximum_select_fusion), channel_id=1, replica_groups=mesh['y_near'=4,'core'=2,'z_pair'=6,'z_bit'=2,'y_far'=2,'x'=4] {'z_pair'}, dimensions={0}, use_global_device_ids=true | all-gather | bytes 917504 | tf_op jit(solution)/shard_map/all_gather | solution.py:90
  58.4 1.5 %convolution_convert_fusion = bf16[384,1024]{1,0:T(8,128)(2,1)} fusion(bf16[384,384]{1,0:T(8,128)(2,1)S(1)} %bitcast.29, bf16[384,1024]{1,0:T(8,128)(2,1)S(1)} %all_gather.9), kind=kOutput, calls=%fused_computation.5 | convolution fusion | flops 302383104 | bytes 1867776 | tf_op jit(solution)/shard_map/dot_general | solution.py:92
  59.9 0.0 all-to-all-done.1
  59.9 6.7 %all-to-all-start.2 = ((bf16[8,48,1024]{2,1,0:T(8,128)(2,1)}), bf16[8,48,1024]{2,1,0:T(8,128)(2,1)}, u32[]{:S(2)}, u32[]{:S(2)}) async-start(bf16[8,48,1024]{2,1,0:T(8,128)(2,1)} %bitcast.4), calls=%async_computation.2 | async-start | bytes 1572864 | tf_op jit(solution)/shard_map/all_to_all | solution.py:57
  66.6 0.2 subtract_reduce_fusion
  66.8 0.0 copy-done.2
  66.8 1.7 %subtract_convert_fusion = (bf16[48,1024]{1,0:T(8,128)(2,1)S(1)}, f32[48,1024]{1,0:T(8,128)}) fusion(f32[48,1024]{1,0:T(8,128)S(1)} %subtract_reduce_fusion, f32[48,1024]{1,0:T(8,128)S(1)} %copy-done.2, f32[48,8192]{1,0:T(8,128)} %param.8, s32[]{:T(128)S(6)} %select_n.11), kind=kLoop, calls=%fused_computation.11 | loop fusion | flops 393216 | bytes 884740 | tf_op jit(solution)/shard_map/convert_element_type | solution.py:102
  68.4 18.5 %all-gather = bf16[384,1024]{1,0:T(8,128)(2,1)S(1)} all-gather(bf16[48,1024]{1,0:T(8,128)(2,1)S(1)} %get-tuple-element.19), channel_id=2, replica_groups=mesh['y_near'=4,'core'=2,'z_pair'=6,'z_bit'=2,'y_far'=2,'x'=4] {'y_near'..., dimensions={0}, use_global_device_ids=true | all-gather | bytes 884736 | tf_op jit(solution)/shard_map/all_gather | solution.py:102
  87.0 1.4 %convert_bitcast_fusion.1 = (f32[48,8,1024]{2,0,1:T(8,128)S(1)}, f32[8,6,8,1024]{3,2,1,0:T(8,128)}) fusion(bf16[8,48,1024]{2,1,0:T(8,128)(2,1)S(1)} %bitcast.27), kind=kLoop, calls=%fused_computation.1 | loop fusion | flops 393216 | bytes 3932160 | tf_op jit(solution)/shard_map/convert_element_type | solution.py:103
  88.3 0.9 copy.19
  89.2 0.3 reshape.57
  89.5 0.0 copy-start.1
  89.5 2.8 %copy.21 = f32[8,6,8,1024]{3,2,0,1:T(8,128)} copy(f32[8,6,8,1024]{3,2,1,0:T(8,128)} %get-tuple-element.22) | data formatting | bytes 3145728 | tf_op jit(solution)/shard_map/convert_element_type | solution.py:103
  92.3 0.0 copy-done.1
  92.4 1.1 %multiply_convert_fusion = bf16[1,48,8192]{2,1,0:T(8,128)(2,1)} fusion(f32[1,48,8192]{2,1,0:T(8,128)S(1)} %reshape.57, bf16[1,48,8192]{2,1,0:T(8,128)(2,1)S(1)} %copy-done.1), kind=kLoop, calls=%fused_computation.3 | loop fusion | flops 1572864 | bytes 3145728 | tf_op jit(solution)/shard_map/convert_element_type | solution.py:104
  93.4 0.0 all-to-all-done.2
  93.4 1.3 %convert_reduce_fusion = f32[48,1024]{1,0:T(8,128)S(1)} fusion(bf16[8,48,1024]{2,1,0:T(8,128)(2,1)} %all-to-all-done.2), kind=kLoop, calls=%fused_computation.2 | loop fusion | flops 737280 | bytes 983040 | tf_op jit(solution)/shard_map/reduce_sum | solution.py:106
  94.7 0.0 copy-done.3
  94.7 0.9 multiply_subtract_fusion
  (7 shorter events, 0.0 us)
Async XLA Ops:
  0.6 18.1 %copy-start.6 = (bf16[1,32,1024]{2,1,0:T(8,128)(2,1)S(1)}, bf16[1,32,1024]{2,1,0:T(8,128)(2,1)}, u32[]{:S(2)}) copy-start(bf16[1,32,1024]{2,1,0:T(8,128)(2,1)} %param.12) | copy-start | bytes 196612
  0.6 16.2 %copy-start = (bf16[1,48,8192]{2,1,0:T(8,128)(2,1)S(1)}, bf16[1,48,8192]{2,1,0:T(8,128)(2,1)}, u32[]{:S(2)}) copy-start(bf16[1,48,8192]{2,1,0:T(8,128)(2,1)} %param.9) | copy-start | bytes 2359300
  2.7 16.1 %all-to-all-start = ((bf16[8,48,384]{2,1,0:T(8,128)(2,1)}), bf16[8,48,384]{2,1,0:T(8,128)(2,1)S(1)}, u32[]{:S(2)}, u32[]{:S(2)}) async-start(bf16[8,48,384]{2,1,0:T(8,128)(2,1)} %pack.1), calls=%async_computation | async-start | bytes 589824 | tf_op jit(solution)/shard_map/all_to_all | solution.py:57
  9.4 9.4 %collective-permute-start = (bf16[32,1024]{1,0:T(8,128)(2,1)}, bf16[32,1024]{1,0:T(8,128)(2,1)S(1)}, u32[]{:S(2)}, u32[]{:S(2)}) collective-permute-start(bf16[32,1024]{1,0:T(8,128)(2,1)} %bitcast.31), channel_id=1, source_target_pairs={{0,4},{4,0},{1,5},{5,1},{2,6},{6,2},{3,7},{7,3},{8,12},{12,8},{9,1... | collective-permute-start | bytes 196616 | tf_op jit(solution)/shard_map/ppermute | solution.py:76
  20.1 39.8 %all-to-all-start.1 = ((bf16[8,48,1024]{2,1,0:T(8,128)(2,1)}), bf16[8,48,1024]{2,1,0:T(8,128)(2,1)S(1)}, u32[]{:S(2)}, u32[]{:S(2)}) async-start(bf16[8,48,1024]{2,1,0:T(8,128)(2,1)} %copy.18), calls=%async_computation.1 | async-start | bytes 1572864 | tf_op jit(solution)/shard_map/all_to_all | solution.py:57
  59.9 6.9 %copy-start.2 = (f32[48,1024]{1,0:T(8,128)S(1)}, f32[48,1024]{1,0:T(8,128)}, u32[]{:S(2)}) copy-start(f32[48,1024]{1,0:T(8,128)} %param.10) | copy-start | bytes 589828
  59.9 33.6 %all-to-all-start.2 = ((bf16[8,48,1024]{2,1,0:T(8,128)(2,1)}), bf16[8,48,1024]{2,1,0:T(8,128)(2,1)}, u32[]{:S(2)}, u32[]{:S(2)}) async-start(bf16[8,48,1024]{2,1,0:T(8,128)(2,1)} %bitcast.4), calls=%async_computation.2 | async-start | bytes 1572864 | tf_op jit(solution)/shard_map/all_to_all | solution.py:57
  89.5 2.8 %copy-start.1 = (bf16[1,48,8192]{2,1,0:T(8,128)(2,1)S(1)}, bf16[1,48,8192]{2,1,0:T(8,128)(2,1)}, u32[]{:S(2)}) copy-start(bf16[1,48,8192]{2,1,0:T(8,128)(2,1)} %param.9) | copy-start | bytes 2359300
  92.3 2.4 %copy-start.3 = (f32[1,48,1024]{2,1,0:T(8,128)S(1)}, f32[1,48,1024]{2,1,0:T(8,128)}, u32[]{:S(2)}) copy-start(f32[1,48,1024]{2,1,0:T(8,128)} %param.13) | copy-start | bytes 589828
  92.3 2.4 %copy-start.4 = (f32[1,48,1024]{2,1,0:T(8,128)S(1)}, f32[1,48,1024]{2,1,0:T(8,128)}, u32[]{:S(2)}) copy-start(f32[1,48,1024]{2,1,0:T(8,128)} %param.14) | copy-start | bytes 589828
  92.3 2.4 %copy-start.5 = (f32[1,48,1024]{2,1,0:T(8,128)S(1)}, f32[1,48,1024]{2,1,0:T(8,128)}, u32[]{:S(2)}) copy-start(f32[1,48,1024]{2,1,0:T(8,128)} %param.15) | copy-start | bytes 589828

commit v2 on v1

--- a/solution.py
+++ b/solution.py
@@ -53,6 +53,103 @@
     )(features)
 
 
+def split_kernel(rows_ref, out_ref, sems):
+    count, _, part = out_ref.shape
+    copies = [
+        pltpu.make_async_copy(rows_ref.at[:, pl.ds(j * part, part)], out_ref.at[j], sems.at[j])
+        for j in range(count)
+    ]
+    for copy in copies:
+        copy.start()
+    for copy in copies:
+        copy.wait()
+
+
+def split_by_column(rows, part):
+    height, width = rows.shape
+    return pl.pallas_call(
+        split_kernel,
+        in_specs=[pl.BlockSpec(memory_space=pltpu.VMEM)],
+        out_specs=pl.BlockSpec(memory_space=pl.ANY),
+        out_shape=jax.ShapeDtypeStruct((width // part, height, part), rows.dtype),
+        scratch_shapes=[pltpu.SemaphoreType.DMA((width // part,))],
+        name="split",
+    )(rows)
+
+
+def finish_kernel(
+    moved_ref,
+    rows_ref,
+    parts_ref,
+    weight_ref,
+    first_ref,
+    second_ref,
+    anchor_out,
+    merged_out,
+    weight_out,
+    first_out,
+    second_out,
+    anchor_buf,
+    merged_buf,
+    state_buf,
+    sems,
+):
+    count, height, part = moved_ref.shape
+    copies = []
+
+    def send(source, target):
+        copy = pltpu.make_async_copy(source, target, sems.at[len(copies)])
+        copy.start()
+        copies.append(copy)
+
+    for j in range(count):
+        columns = pl.ds(j * part, part)
+        new_anchor = moved_ref[j].astype(jnp.float32)
+        anchor_buf[:, columns] = new_anchor
+        send(anchor_buf.at[:, columns], anchor_out.at[:, columns])
+        merged = blend_keep * rows_ref[:, columns].astype(jnp.float32) + (1.0 - blend_keep) * new_anchor
+        merged_buf[:, columns] = merged.astype(jnp.bfloat16)
+        send(merged_buf.at[:, columns], merged_out.at[:, columns])
+    for top in range(0, height, 16):
+        lines = pl.ds(top, 16)
+        gradient = parts_ref[0, lines].astype(jnp.float32)
+        for k in range(1, parts_ref.shape[0]):
+            gradient = gradient + parts_ref[k, lines].astype(jnp.float32)
+        new_first = decay_first * first_ref[lines] + (1.0 - decay_first) * gradient
+        new_second = decay_second * second_ref[lines] + (1.0 - decay_second) * gradient * gradient
+        stepped = new_first / first_fix / (jnp.sqrt(new_second / second_fix) + epsilon)
+        weight = weight_ref[lines]
+        state_buf[0, lines] = weight - inner_rate * (stepped + weight_decay * weight)
+        state_buf[1, lines] = new_first
+        state_buf[2, lines] = new_second
+    send(state_buf.at[0], weight_out)
+    send(state_buf.at[1], first_out)
+    send(state_buf.at[2], second_out)
+    for copy in copies:
+        copy.wait()
+
+
+def finish(moved, rows, parts, weight, first, second):
+    height, width = rows.shape
+    whole = jax.ShapeDtypeStruct((height, width), jnp.float32)
+    state = jax.ShapeDtypeStruct(weight.shape, jnp.float32)
+    kept = pl.BlockSpec(memory_space=pltpu.VMEM)
+    far = pl.BlockSpec(memory_space=pl.ANY)
+    return pl.pallas_call(
+        finish_kernel,
+        in_specs=[kept] * 6,
+        out_specs=[far] * 5,
+        out_shape=[whole, jax.ShapeDtypeStruct(rows.shape, rows.dtype), state, state, state],
+        scratch_shapes=[
+            pltpu.VMEM((height, width), jnp.float32),
+            pltpu.VMEM((height, width), jnp.bfloat16),
+            pltpu.VMEM((3, *weight.shape), jnp.float32),
+            pltpu.SemaphoreType.DMA((2 * moved.shape[0] + 3,)),
+        ],
+        name="finish",
+    )(moved, rows, parts, weight, first, second)
+
+
 def exchange(x, axes):
     return lax.all_to_all(x, axes, 0, 0, tiled=True)
 
@@ -69,46 +166,38 @@
 ):
     replicas = lax.axis_size(REPLICA)
     rows = replica_rows[0]
-    height, width = rows.shape
+    height, _ = rows.shape
     part = outer_velocity.shape[1]
-
+    mine = cotangent[0]
+
+    other = lax.ppermute(mine, "y_far", [(0, 1), (1, 0)])
     packed = packed_by_token(features[0])
-    other = lax.ppermute(cotangent[0], "y_far", [(0, 1), (1, 0)])
     own_tokens = exchange(packed, GROUP)
+
+    pieces = split_by_column(rows, part)
+    offset = lax.axis_index(REPLICA) * part
+    anchor_part = lax.dynamic_slice_in_dim(anchor, offset, part, 1)
+    both = jnp.where(lax.axis_index("y_far") == 0, jnp.concatenate([mine, other]), jnp.concatenate([other, mine]))
+    pieces, own_tokens, both, anchor_part = lax.optimization_barrier((pieces, own_tokens, both, anchor_part))
+
+    pieces = exchange(pieces, REPLICA)
+
+    own_cotangent = lax.all_gather(both, "z_pair", axis=0, tiled=True)
     own_tokens = own_tokens.reshape(-1, own_tokens.shape[-1])
-
-    first = lax.axis_index("y_far") == 0
-    both = jnp.where(
-        first,
-        jnp.concatenate([cotangent[0], other]),
-        jnp.concatenate([other, cotangent[0]]),
-    )
-    pieces = jnp.moveaxis(rows.reshape(height, replicas, part), 1, 0)
-    pieces, own_tokens, both = lax.optimization_barrier((pieces, own_tokens, both))
-    pieces = exchange(pieces, REPLICA)
-
-    own_cotangent = lax.all_gather(both, "z_pair", axis=0, tiled=True)
-
     partial = jnp.dot(own_tokens, own_cotangent, preferred_element_type=jnp.float32)
     partial = partial.astype(jnp.bfloat16).reshape(-1, height, partial.shape[1])
     partial, pieces = lax.optimization_barrier((partial, pieces))
     parts = exchange(partial, GROUP)
 
-    offset = lax.axis_index(REPLICA) * part
-    anchor_part = lax.dynamic_slice_in_dim(anchor, offset, part, 1)
     outer_grad = jnp.sum(anchor_part[None] - pieces.astype(jnp.float32), axis=0) / replicas
     new_velocity = momentum_keep * outer_velocity + outer_grad
     moved = anchor_part - outer_rate * (outer_grad + momentum_keep * new_velocity)
     moved = lax.all_gather(moved.astype(jnp.bfloat16), REPLICA, axis=0)
-    new_anchor = jnp.moveaxis(moved, 0, 1).reshape(height, width).astype(jnp.float32)
-    merged_rows = (blend_keep * rows.astype(jnp.float32) + (1.0 - blend_keep) * new_anchor).astype(jnp.bfloat16)
-
-    gradient = jnp.sum(parts.astype(jnp.float32), axis=0)[None]
-    new_first = decay_first * first_moment + (1.0 - decay_first) * gradient
-    new_second = decay_second * second_moment + (1.0 - decay_second) * gradient * gradient
-    stepped = new_first / first_fix / (jnp.sqrt(new_second / second_fix) + epsilon)
-    new_weight = inner_weight - inner_rate * (stepped + weight_decay * inner_weight)
-    return (new_anchor, merged_rows[None], new_velocity, new_weight, new_first, new_second)
+
+    new_anchor, merged_rows, new_weight, new_first, new_second = finish(
+        moved, rows, parts, inner_weight[0], first_moment[0], second_moment[0]
+    )
+    return (new_anchor, merged_rows[None], new_velocity, new_weight[None], new_first[None], new_second[None])
 
 
 def solution(mesh):

time: 97.3 us -> 90.7 us (0.932)
  local copies, waits for them, and re-layouts: 6.73 us -> 0.96 us
  Pallas kernels: 2.05 us -> 7.68 us
  other arithmetic: 6.46 us -> 0.92 us
  waiting for transfers between devices: 1.46 us -> 0.01 us
  blocking collectives: 44.3 us -> 45.3 us
    pallas_call x0 -> x2, Pallas kernels: none -> 5.59 us  [the longest x1 3.52 us: finish(): pl.pallas_call(finish_kernel, in_specs=[kept] * 6, out_specs=[far] * 5, o...]
    convert_element_type x3 -> x0, local copies, waits for them, and re-layouts: 4 us -> none  [local(): jnp.moveaxis(moved, 0, 1).reshape(height, width).astype(jnp.float32)]
    convert_element_type x2 -> x0, other arithmetic: 2.45 us -> none  [the longest x1 1.37 us: local(): jnp.moveaxis(moved, 0, 1).reshape(height, width).astype(jnp.float32)]
    ppermute x1, waiting for transfers between devices: 1.45 us -> 0.01 us  [local(): other = lax.ppermute(mine, 'y_far', [(0, 1), (1, 0)])]
    optimization_barrier x1 -> x0, local copies, waits for them, and re-layouts: 1.32 us -> none  [local(): lax.optimization_barrier((pieces, own_tokens, both))]
    reduce_sum x1 -> x0, other arithmetic: 1.27 us -> none  [local(): gradient = jnp.sum(parts.astype(jnp.float32), axis=0)[None]]
    all_gather x1, blocking collectives: 18.5 us -> 19.5 us  [local(): moved = lax.all_gather(moved.astype(jnp.bfloat16), REPLICA, axis=0)]
  transfers between devices with their start and end apart: 4 -> 4, of which waited for: 1 -> 0; matrix products, arithmetic and copies ran while one was open for 12% -> 3% of each run, Pallas kernels for 0% -> 2%
where the time goes in v2:
time: 90.7 us; the launch traced here: 89.3 us
  blocking collectives  45.3 us (50%)
  starting transfers between devices  32.3 us (36%)
  Pallas kernels  7.68 us (8%)
  matrix products  1.46 us (2%)
  local copies, waits for them, and re-layouts  0.96 us (1%)
  other arithmetic  0.92 us (1%)
    all_gather x1, blocking collectives, local(): own_cotangent = lax.all_gather(both, 'z_pair', axis=0, tiled=True)  25.8 us
    all_to_all x3, starting transfers between devices, exchange(): return lax.all_to_all(x, axes, 0, 0, tiled=True)  24.9 us
    all_gather x1, blocking collectives, local(): moved = lax.all_gather(moved.astype(jnp.bfloat16), REPLICA, axis=0)  19.5 us
    ppermute x1, starting transfers between devices, local(): other = lax.ppermute(mine, 'y_far', [(0, 1), (1, 0)])  7.44 us
    pallas_call x1, Pallas kernels, finish(): pl.pallas_call(finish_kernel, in_specs=[kept] * 6, out_specs=[far] * 5, o...  3.52 us
    pallas_call x1, Pallas kernels, packed_by_token(): pl.pallas_call(pack_kernel, out_shape=jax.ShapeDtypeStruct((8, rows, toke...  2.1 us
    pallas_call x1, Pallas kernels, split_by_column(): pl.pallas_call(split_kernel, in_specs=[pl.BlockSpec(memory_space=pltpu.VM...  2.07 us
  transfers between devices with their start and end apart: 4, of which 0 were waited for; matrix products, arithmetic and copies ran while one was open for 3% of the time, Pallas kernels for 2%

profile of v2, /device:TPU:1, one launch (start us, length us, event | category | flops | bytes accessed | tf_op | source)
XLA Modules:
  0.0 89.3 jit_solution(13350326035042613657)
XLA Ops:
  0.6 0.0 copy-start
  0.6 0.0 copy-start.3
  0.7 2.1 %pack.1 = bf16[8,48,384]{2,1,0:T(8,128)(2,1)} custom-call(bf16[48,3072]{1,0:T(8,128)(2,1)} %bitcast.19), custom_call_target="tpu_custom_call" | custom-call | tf_op jit(solution)/shard_map/pack/pallas_call | solution.py:49
  2.8 6.6 %all-to-all-start = ((bf16[8,48,384]{2,1,0:T(8,128)(2,1)}), bf16[8,48,384]{2,1,0:T(8,128)(2,1)S(1)}, u32[]{:S(2)}, u32[]{:S(2)}) async-start(bf16[8,48,384]{2,1,0:T(8,128)(2,1)} %pack.1), calls=%async_computation | async-start | bytes 589824 | tf_op jit(solution)/shard_map/all_to_all | solution.py:154
  9.4 7.4 %collective-permute-start = (bf16[32,1024]{1,0:T(8,128)(2,1)}, bf16[32,1024]{1,0:T(8,128)(2,1)S(1)}, u32[]{:S(2)}, u32[]{:S(2)}) collective-permute-start(bf16[32,1024]{1,0:T(8,128)(2,1)} %bitcast.23), channel_id=1, source_target_pairs={{0,4},{4,0},{1,5},{5,1},{2,6},{6,2},{3,7},{7,3},{8,12},{12,8},{9,1... | collective-permute-start | bytes 196616 | tf_op jit(solution)/shard_map/ppermute | solution.py:173
  16.9 2.1 %split.1 = bf16[8,48,1024]{2,1,0:T(8,128)(2,1)} custom-call(bf16[48,8192]{1,0:T(8,128)(2,1)} %bitcast.15), custom_call_target="tpu_custom_call" | custom-call | tf_op jit(solution)/shard_map/split/pallas_call | solution.py:70
  18.9 0.0 copy-done
  19.0 0.0 collective-permute-done
  19.0 0.0 copy-done.3
  19.0 0.0 all-to-all-done
  19.1 11.4 %all-to-all-start.1 = ((bf16[8,48,1024]{2,1,0:T(8,128)(2,1)}), bf16[8,48,1024]{2,1,0:T(8,128)(2,1)S(1)}, u32[]{:S(2)}, u32[]{:S(2)}) async-start(bf16[8,48,1024]{2,1,0:T(8,128)(2,1)} %split.1), calls=%async_computation.1 | async-start | bytes 1572864 | tf_op jit(solution)/shard_map/all_to_all | solution.py:154
  30.4 25.8 %all_gather.9 = bf16[384,1024]{1,0:T(8,128)(2,1)S(1)} all-gather(bf16[64,1024]{1,0:T(8,128)(2,1)S(1)} %maximum_select_fusion), channel_id=1, replica_groups=mesh['y_near'=4,'core'=2,'z_pair'=6,'z_bit'=2,'y_far'=2,'x'=4] {'z_pair'}, dimensions={0}, use_global_device_ids=true | all-gather | bytes 917504 | tf_op jit(solution)/shard_map/all_gather | solution.py:185
  56.2 1.5 %convolution_convert_fusion = bf16[384,1024]{1,0:T(8,128)(2,1)} fusion(bf16[384,384]{1,0:T(8,128)(2,1)S(1)} %bitcast.18, bf16[384,1024]{1,0:T(8,128)(2,1)S(1)} %all_gather.9), kind=kOutput, calls=%fused_computation.1 | convolution fusion | flops 302383104 | bytes 1867776 | tf_op jit(solution)/shard_map/dot_general | solution.py:187
  57.7 0.0 copy-start.2
  57.7 0.0 all-to-all-done.1
  57.7 6.8 %all-to-all-start.2 = ((bf16[8,48,1024]{2,1,0:T(8,128)(2,1)}), bf16[8,48,1024]{2,1,0:T(8,128)(2,1)S(1)}, u32[]{:S(2)}, u32[]{:S(2)}) async-start(bf16[8,48,1024]{2,1,0:T(8,128)(2,1)} %bitcast.4), calls=%async_computation.2 | async-start | bytes 1572864 | tf_op jit(solution)/shard_map/all_to_all | solution.py:154
  64.5 0.2 subtract_reduce_fusion
  64.6 0.0 copy-done.2
  64.6 0.7 subtract_convert_fusion
  65.4 19.5 %all-gather = bf16[384,1024]{1,0:T(8,128)(2,1)} all-gather(bf16[48,1024]{1,0:T(8,128)(2,1)S(1)} %get-tuple-element.28), channel_id=2, replica_groups=mesh['y_near'=4,'core'=2,'z_pair'=6,'z_bit'=2,'y_far'=2,'x'=4] {'y_near'..., dimensions={0}, use_global_device_ids=true | all-gather | bytes 884736 | tf_op jit(solution)/shard_map/all_gather | solution.py:195
  84.9 0.0 all-to-all-done.2.parts_ref
  84.9 0.0 copy-start.1
  84.9 0.9 %copy-done.1 = bf16[8,48,1024]{2,1,0:T(8,128)(2,1)} copy-done((bf16[8,48,1024]{2,1,0:T(8,128)(2,1)}, bf16[8,48,1024]{2,1,0:T(8,128)(2,1)S(1)}, u32[]{:S(2)}) %copy-start.1) | copy-done | bytes 786456
  85.8 3.5 %finish.1 = (f32[48,8192]{1,0:T(8,128)}, bf16[48,8192]{1,0:T(8,128)(2,1)}, f32[48,1024]{1,0:T(8,128)}, f32[48,1024]{1,0:T(8,128)}, f32[48,1024]{1,0:T(8,128)}) custom-call(bf16[8,48,1024]{2,1,0:T(8,128)(2,1)} %bitcast.17, bf16[48,8192]{1,0:T(8,128)(2,1)} %bitcast.16, bf16[8,48,1024]{2,1,0:T(8,128)(2,1)} %copy-done.1, f32[48,1024]{1,0:T(8,128)} %bitcast.20, ...), custom_call_target="tpu_custom_call" | custom-call | tf_op jit(solution)/shard_map/finish/pallas_call | solution.py:138
  (2 shorter events, 0.1 us)
Async XLA Ops:
  0.6 18.3 %copy-start = (f32[48,8192]{1,0:T(8,128)S(1)}, f32[48,8192]{1,0:T(8,128)}, u32[]{:S(2)}) copy-start(f32[48,8192]{1,0:T(8,128)} %param.8) | copy-start | bytes 4718596
  0.6 18.4 %copy-start.3 = (bf16[1,32,1024]{2,1,0:T(8,128)(2,1)S(1)}, bf16[1,32,1024]{2,1,0:T(8,128)(2,1)}, u32[]{:S(2)}) copy-start(bf16[1,32,1024]{2,1,0:T(8,128)(2,1)} %param.12) | copy-start | bytes 196612
  2.8 16.3 %all-to-all-start = ((bf16[8,48,384]{2,1,0:T(8,128)(2,1)}), bf16[8,48,384]{2,1,0:T(8,128)(2,1)S(1)}, u32[]{:S(2)}, u32[]{:S(2)}) async-start(bf16[8,48,384]{2,1,0:T(8,128)(2,1)} %pack.1), calls=%async_computation | async-start | bytes 589824 | tf_op jit(solution)/shard_map/all_to_all | solution.py:154
  9.4 9.6 %collective-permute-start = (bf16[32,1024]{1,0:T(8,128)(2,1)}, bf16[32,1024]{1,0:T(8,128)(2,1)S(1)}, u32[]{:S(2)}, u32[]{:S(2)}) collective-permute-start(bf16[32,1024]{1,0:T(8,128)(2,1)} %bitcast.23), channel_id=1, source_target_pairs={{0,4},{4,0},{1,5},{5,1},{2,6},{6,2},{3,7},{7,3},{8,12},{12,8},{9,1... | collective-permute-start | bytes 196616 | tf_op jit(solution)/shard_map/ppermute | solution.py:173
  19.1 38.6 %all-to-all-start.1 = ((bf16[8,48,1024]{2,1,0:T(8,128)(2,1)}), bf16[8,48,1024]{2,1,0:T(8,128)(2,1)S(1)}, u32[]{:S(2)}, u32[]{:S(2)}) async-start(bf16[8,48,1024]{2,1,0:T(8,128)(2,1)} %split.1), calls=%async_computation.1 | async-start | bytes 1572864 | tf_op jit(solution)/shard_map/all_to_all | solution.py:154
  57.7 7.0 %copy-start.2 = (f32[48,1024]{1,0:T(8,128)S(1)}, f32[48,1024]{1,0:T(8,128)}, u32[]{:S(2)}) copy-start(f32[48,1024]{1,0:T(8,128)} %param.10) | copy-start | bytes 589828
  57.7 27.2 %all-to-all-start.2 = ((bf16[8,48,1024]{2,1,0:T(8,128)(2,1)}), bf16[8,48,1024]{2,1,0:T(8,128)(2,1)S(1)}, u32[]{:S(2)}, u32[]{:S(2)}) async-start(bf16[8,48,1024]{2,1,0:T(8,128)(2,1)} %bitcast.4), calls=%async_computation.2 | async-start | bytes 1572864 | tf_op jit(solution)/shard_map/all_to_all | solution.py:154
  84.9 0.9 %copy-start.1 = (bf16[8,48,1024]{2,1,0:T(8,128)(2,1)}, bf16[8,48,1024]{2,1,0:T(8,128)(2,1)S(1)}, u32[]{:S(2)}) copy-start(bf16[8,48,1024]{2,1,0:T(8,128)(2,1)S(1)} %all-to-all-done.2.parts_ref) | copy-start | bytes 2359300

commit v3 on v1

--- a/solution.py
+++ b/solution.py
@@ -25,32 +25,69 @@
 LANES = 128
 
 
-def pack_kernel(features_ref, out_ref):
-    rows, tokens = features_ref.shape
+def start_all(copies):
+    for copy in copies:
+        copy.start()
+    return copies
+
+
+def prepare_kernel(
+    features_ref, rows_ref, packed_out, pieces_out, features_buf, rows_buf, packed_buf, in_sems, out_sems
+):
+    height, tokens = features_ref.shape
+    count, _, part = pieces_out.shape
+    features_in = pltpu.make_async_copy(features_ref, features_buf, in_sems.at[count])
+    features_in.start()
+    columns = [pl.ds(j * part, part) for j in range(count)]
+    rows_in = start_all(
+        [pltpu.make_async_copy(rows_ref.at[:, columns[j]], rows_buf.at[:, columns[j]], in_sems.at[j]) for j in range(count)]
+    )
     piece = LANES // 4
-    lane = lax.broadcasted_iota(jnp.int32, (rows, LANES), 1)
+    lane = lax.broadcasted_iota(jnp.int32, (height, LANES), 1)
+    features_in.wait()
     for block in range(tokens // (8 * LANES)):
         for bit in range(2):
             tiles = []
             for place in range(4):
                 column = (block * 2 + place // 2) * 4 + bit * 2 + place % 2
-                tiles.append(features_ref[:, column * LANES : (column + 1) * LANES].astype(jnp.float32))
+                tiles.append(features_buf[:, column * LANES : (column + 1) * LANES].astype(jnp.float32))
             for x in range(4):
-                packed = jnp.zeros((rows, LANES), jnp.float32)
+                packed = jnp.zeros((height, LANES), jnp.float32)
                 for place in range(4):
                     shift = (place - x) * piece % LANES
                     turned = pltpu.roll(tiles[place], shift, 1) if shift else tiles[place]
                     packed = jnp.where(lane // piece == place, turned, packed)
-                out_ref[bit * 4 + x, :, block * LANES : (block + 1) * LANES] = packed.astype(jnp.bfloat16)
+                packed_buf[bit * 4 + x, :, block * LANES : (block + 1) * LANES] = packed.astype(jnp.bfloat16)
+    copies = start_all([pltpu.make_async_copy(packed_buf, packed_out, out_sems.at[count])])
+    for j in range(count):
+        rows_in[j].wait()
+        copies += start_all([pltpu.make_async_copy(rows_buf.at[:, columns[j]], pieces_out.at[j], out_sems.at[j])])
+    for copy in copies:
+        copy.wait()
 
 
-def packed_by_token(features):
-    rows, tokens = features.shape
+def prepare(features, rows, part):
+    height, width = rows.shape
+    tokens = features.shape[1]
+    count = width // part
+    far = pl.BlockSpec(memory_space=pl.ANY)
     return pl.pallas_call(
-        pack_kernel,
-        out_shape=jax.ShapeDtypeStruct((8, rows, tokens // 8), jnp.bfloat16),
-        name="pack",
-    )(features)
+        prepare_kernel,
+        in_specs=[far] * 2,
+        out_specs=[far] * 2,
+        out_shape=[
+            jax.ShapeDtypeStruct((8, height, tokens // 8), jnp.bfloat16),
+            jax.ShapeDtypeStruct((count, height, part), rows.dtype),
+        ],
+        scratch_shapes=[
+            pltpu.VMEM(features.shape, features.dtype),
+            pltpu.VMEM(rows.shape, rows.dtype),
+            pltpu.VMEM((8, height, tokens // 8), jnp.bfloat16),
+            pltpu.SemaphoreType.DMA((count + 1,)),
+            pltpu.SemaphoreType.DMA((count + 1,)),
+        ],
+        name="prepare",
+    )(features, rows)
 
 
 def exchange(x, axes):
@@ -69,38 +106,38 @@
 ):
     replicas = lax.axis_size(REPLICA)
     rows = replica_rows[0]
-    height, width = rows.shape
+    height, _ = rows.shape
     part = outer_velocity.shape[1]
+    mine = cotangent[0]
 
-    packed = packed_by_token(features[0])
-    other = lax.ppermute(cotangent[0], "y_far", [(0, 1), (1, 0)])
+    packed, pieces = prepare(features[0], rows, part)
     own_tokens = exchange(packed, GROUP)
-    own_tokens = own_tokens.reshape(-1, own_tokens.shape[-1])
+    other = lax.ppermute(mine, "y_far", [(0, 1), (1, 0)])
 
-    first = lax.axis_index("y_far") == 0
-    both = jnp.where(
-        first,
-        jnp.concatenate([cotangent[0], other]),
-        jnp.concatenate([other, cotangent[0]]),
-    )
-    pieces = jnp.moveaxis(rows.reshape(height, replicas, part), 1, 0)
-    pieces, own_tokens, both = lax.optimization_barrier((pieces, own_tokens, both))
+    offset = lax.axis_index(REPLICA) * part
+    anchor_part = lax.dynamic_slice_in_dim(anchor, offset, part, 1)
+    pieces, own_tokens, anchor_part = lax.optimization_barrier((pieces, own_tokens, anchor_part))
+
     pieces = exchange(pieces, REPLICA)
 
+    both = jnp.where(
+        lax.axis_index("y_far") == 0,
+        jnp.concatenate([mine, other]),
+        jnp.concatenate([other, mine]),
+    )
     own_cotangent = lax.all_gather(both, "z_pair", axis=0, tiled=True)
-
+    own_tokens = own_tokens.reshape(-1, own_tokens.shape[-1])
     partial = jnp.dot(own_tokens, own_cotangent, preferred_element_type=jnp.float32)
     partial = partial.astype(jnp.bfloat16).reshape(-1, height, partial.shape[1])
     partial, pieces = lax.optimization_barrier((partial, pieces))
     parts = exchange(partial, GROUP)
 
-    offset = lax.axis_index(REPLICA) * part
-    anchor_part = lax.dynamic_slice_in_dim(anchor, offset, part, 1)
     outer_grad = jnp.sum(anchor_part[None] - pieces.astype(jnp.float32), axis=0) / replicas
     new_velocity = momentum_keep * outer_velocity + outer_grad
     moved = anchor_part - outer_rate * (outer_grad + momentum_keep * new_velocity)
-    moved = lax.all_gather(moved.astype(jnp.bfloat16), REPLICA, axis=0)
-    new_anchor = jnp.moveaxis(moved, 0, 1).reshape(height, width).astype(jnp.float32)
+    moved = lax.all_gather(moved.astype(jnp.bfloat16), REPLICA, axis=1, tiled=True)
+
+    new_anchor = moved.astype(jnp.float32)
     merged_rows = (blend_keep * rows.astype(jnp.float32) + (1.0 - blend_keep) * new_anchor).astype(jnp.bfloat16)
 
     gradient = jnp.sum(parts.astype(jnp.float32), axis=0)[None]

time: 97.3 us -> 105 us (1.079)
  waiting for transfers between devices: 1.46 us -> 20.2 us
  starting transfers between devices: 32.4 us -> 24 us
  local copies, waits for them, and re-layouts: 6.73 us -> 0.05 us
  blocking collectives: 44.3 us -> 50.6 us
  other arithmetic: 6.46 us -> 4.5 us
    ppermute x1, waiting for transfers between devices: 1.45 us -> 14 us  [local(): other = lax.ppermute(mine, 'y_far', [(0, 1), (1, 0)])]
    all_to_all x3, waiting for transfers between devices: 0.01 us -> 6.18 us  [exchange(): return lax.all_to_all(x, axes, 0, 0, tiled=True)]
    ppermute x1, starting transfers between devices: 7.44 us -> 1.91 us  [local(): other = lax.ppermute(mine, 'y_far', [(0, 1), (1, 0)])]
    all_gather x1, blocking collectives: 25.8 us -> 31.1 us  [local(): own_cotangent = lax.all_gather(both, 'z_pair', axis=0, tiled=True)]
    convert_element_type x3 -> x0, local copies, waits for them, and re-layouts: 4 us -> none  [local(): jnp.moveaxis(moved, 0, 1).reshape(height, width).astype(jnp.float32)]
    convert_element_type x3 -> x1, other arithmetic: 4.12 us -> 0.73 us  [local(): moved.astype(jnp.bfloat16)]
    all_to_all x3, starting transfers between devices: 25 us -> 22.1 us  [exchange(): return lax.all_to_all(x, axes, 0, 0, tiled=True)]
    broadcast_in_dim x0 -> x1, other arithmetic: none -> 1.65 us  [local(): merged_rows[None]]
  transfers between devices with their start and end apart: 4 -> 4, of which waited for: 1 -> 2; matrix products, arithmetic and copies ran while one was open for 12% -> 4% of each run, Pallas kernels for 0% -> 0%
where the time goes in v3:
time: 105 us; the launch traced here: 104 us
  blocking collectives  50.6 us (48%)
  starting transfers between devices  24 us (23%)
  waiting for transfers between devices  20.2 us (19%)
  other arithmetic  4.5 us (4%)
  Pallas kernels  2.5 us (2%)
  matrix products  1.47 us (1%)
    all_gather x1, blocking collectives, local(): own_cotangent = lax.all_gather(both, 'z_pair', axis=0, tiled=True)  31.1 us
    all_to_all x3, starting transfers between devices, exchange(): return lax.all_to_all(x, axes, 0, 0, tiled=True)  22.1 us
    all_gather x1, blocking collectives, local(): lax.all_gather(moved.astype(jnp.bfloat16), REPLICA, axis=1, tiled=True)  19.5 us
    ppermute x1, waiting for transfers between devices, local(): other = lax.ppermute(mine, 'y_far', [(0, 1), (1, 0)])  14 us
    all_to_all x3, waiting for transfers between devices, exchange(): return lax.all_to_all(x, axes, 0, 0, tiled=True)  6.18 us
    pallas_call x1, Pallas kernels, prepare(): pl.pallas_call(prepare_kernel, in_specs=[far] * 2, out_specs=[far] * 2, o...  2.5 us
  transfers between devices with their start and end apart: 4, of which 2 were waited for; matrix products, arithmetic and copies ran while one was open for 4% of the time, Pallas kernels for 0%

profile of v3, /device:TPU:1, one launch (start us, length us, event | category | flops | bytes accessed | tf_op | source)
XLA Modules:
  0.0 104.1 jit_solution(8983366676764569)
XLA Ops:
  0.6 0.0 copy-start
  0.6 0.0 copy-start.5
  0.7 2.5 %prepare.1 = (bf16[8,48,384]{2,1,0:T(8,128)(2,1)}, bf16[8,48,1024]{2,1,0:T(8,128)(2,1)}) custom-call(bf16[48,3072]{1,0:T(8,128)(2,1)} %bitcast.19, bf16[48,8192]{1,0:T(8,128)(2,1)} %bitcast.17), custom_call_target="tpu_custom_call" | custom-call | tf_op jit(solution)/shard_map/prepare/pallas_call | solution.py:74
  3.2 6.7 %all-to-all-start = ((bf16[8,48,384]{2,1,0:T(8,128)(2,1)}), bf16[8,48,384]{2,1,0:T(8,128)(2,1)S(1)}, u32[]{:S(2)}, u32[]{:S(2)}) async-start(bf16[8,48,384]{2,1,0:T(8,128)(2,1)} %get-tuple-element.14), calls=%async_computation | async-start | bytes 589824 | tf_op jit(solution)/shard_map/all_to_all | solution.py:94
  9.8 0.0 copy-done
  9.9 6.2 %all-to-all-done = bf16[8,48,384]{2,1,0:T(8,128)(2,1)S(1)} async-done(((bf16[8,48,384]{2,1,0:T(8,128)(2,1)}), bf16[8,48,384]{2,1,0:T(8,128)(2,1)S(1)}, u32[]{:S(2)}, u32[]{:S(2)}) %all-to-all-start) | async-done | bytes 294944 | tf_op jit(solution)/shard_map/all_to_all | solution.py:94
  16.0 11.8 %all-to-all-start.1 = ((bf16[8,48,1024]{2,1,0:T(8,128)(2,1)}), bf16[8,48,1024]{2,1,0:T(8,128)(2,1)S(1)}, u32[]{:S(2)}, u32[]{:S(2)}) async-start(bf16[8,48,1024]{2,1,0:T(8,128)(2,1)} %get-tuple-element.17), calls=%async_computation.1 | async-start | bytes 1572864 | tf_op jit(solution)/shard_map/all_to_all | solution.py:94
  27.8 0.0 copy-done.5
  27.8 1.9 %collective-permute-start = (bf16[32,1024]{1,0:T(8,128)(2,1)S(1)}, bf16[32,1024]{1,0:T(8,128)(2,1)S(1)}, u32[]{:S(2)}, u32[]{:S(2)}) collective-permute-start(bf16[32,1024]{1,0:T(8,128)(2,1)S(1)} %bitcast.20), channel_id=1, source_target_pairs={{0,4},{4,0},{1,5},{5,1},{2,6},{6,2},{3,7},{7,3},{8,12},{12,8},{9,1... | collective-permute-start | bytes 196616 | tf_op jit(solution)/shard_map/ppermute | solution.py:115
  29.8 14.0 %collective-permute-done = bf16[32,1024]{1,0:T(8,128)(2,1)S(1)} collective-permute-done((bf16[32,1024]{1,0:T(8,128)(2,1)S(1)}, bf16[32,1024]{1,0:T(8,128)(2,1)S(1)}, u32[]{:S(2)}, u32[]{:S(2)}) %collective-permute-start) | collective-permute-done | bytes 65568 | tf_op jit(solution)/shard_map/ppermute | solution.py:115
  43.8 31.1 %all_gather.6 = bf16[384,1024]{1,0:T(8,128)(2,1)S(1)} all-gather(bf16[64,1024]{1,0:T(8,128)(2,1)S(1)} %maximum_select_fusion), channel_id=1, replica_groups=mesh['y_near'=4,'core'=2,'z_pair'=6,'z_bit'=2,'y_far'=2,'x'=4] {'z_pair'}, dimensions={0}, use_global_device_ids=true | all-gather | bytes 917504 | tf_op jit(solution)/shard_map/all_gather | solution.py:128
  74.9 1.5 %convolution_convert_fusion = bf16[384,1024]{1,0:T(8,128)(2,1)} fusion(bf16[384,384]{1,0:T(8,128)(2,1)S(1)} %bitcast.18, bf16[384,1024]{1,0:T(8,128)(2,1)S(1)} %all_gather.6), kind=kOutput, calls=%fused_computation.3 | convolution fusion | flops 302383104 | bytes 1867776 | tf_op jit(solution)/shard_map/dot_general | solution.py:130
  76.4 0.0 copy-start.2
  76.4 0.0 all-to-all-done.1
  76.4 3.7 %all-to-all-start.2 = ((bf16[8,48,1024]{2,1,0:T(8,128)(2,1)}), bf16[8,48,1024]{2,1,0:T(8,128)(2,1)S(1)}, u32[]{:S(2)}, u32[]{:S(2)}) async-start(bf16[8,48,1024]{2,1,0:T(8,128)(2,1)} %bitcast.4), calls=%async_computation.2 | async-start | bytes 1572864 | tf_op jit(solution)/shard_map/all_to_all | solution.py:94
  80.1 0.0 copy-start.1
  80.1 0.2 subtract_reduce_fusion
  80.3 0.0 copy-done.2
  80.3 0.7 subtract_convert_fusion
  81.0 19.5 %all_gather.7 = bf16[48,8192]{1,0:T(8,128)(2,1)S(1)} all-gather(bf16[48,1024]{1,0:T(8,128)(2,1)S(1)} %get-tuple-element.25), channel_id=1, replica_groups=mesh['y_near'=4,'core'=2,'z_pair'=6,'z_bit'=2,'y_far'=2,'x'=4] {'y_near'..., dimensions={1}, use_global_device_ids=true | all-gather | bytes 884736 | tf_op jit(solution)/shard_map/all_gather | solution.py:138
  100.5 0.0 copy-done.1
  100.5 0.0 copy-start.3
  100.5 0.0 copy-start.4
  100.5 1.7 %fusion = (bf16[1,48,8192]{2,1,0:T(8,128)(2,1)}, f32[48,8192]{1,0:T(8,128)}) fusion(bf16[1,48,8192]{2,1,0:T(8,128)(2,1)S(1)} %copy-done.1, bf16[48,8192]{1,0:T(8,128)(2,1)S(1)} %all_gather.7), kind=kLoop, calls=%fused_computation.4 | loop fusion | flops 1966080 | bytes 3932160 | tf_op jit(solution)/shard_map/broadcast_in_dim | solution.py:148
  102.1 0.0 all-to-all-done.2
  102.1 0.1 convert_reduce_fusion
  102.3 0.0 copy-done.3
  102.3 0.0 copy-done.4
  102.3 1.8 %multiply_subtract_fusion = (f32[1,48,1024]{2,1,0:T(8,128)}, f32[1,48,1024]{2,1,0:T(8,128)}, f32[1,48,1024]{2,1,0:T(8,128)}) fusion(f32[1,48,1024]{2,1,0:T(8,128)S(1)} %copy-done.3, f32[48,1024]{1,0:T(8,128)S(1)} %convert_reduce_fusion, f32[1,48,1024]{2,1,0:T(8,128)S(1)} %copy-done.4, f32[1,48,1024]{2,1,0:T(8,128)} %param.15), kind=kLoop, calls=%fused_computation.9 | loop fusion | flops 737280 | bytes 1376256 | tf_op jit(solution)/shard_map/sub | solution.py:147
  (2 shorter events, 0.0 us)
Async XLA Ops:
  0.6 9.2 %copy-start = (f32[48,8192]{1,0:T(8,128)S(1)}, f32[48,8192]{1,0:T(8,128)}, u32[]{:S(2)}) copy-start(f32[48,8192]{1,0:T(8,128)} %param.8) | copy-start | bytes 4718596
  0.6 27.2 %copy-start.5 = (bf16[1,32,1024]{2,1,0:T(8,128)(2,1)S(1)}, bf16[1,32,1024]{2,1,0:T(8,128)(2,1)}, u32[]{:S(2)}) copy-start(bf16[1,32,1024]{2,1,0:T(8,128)(2,1)} %param.12) | copy-start | bytes 196612
  3.2 12.9 %all-to-all-start = ((bf16[8,48,384]{2,1,0:T(8,128)(2,1)}), bf16[8,48,384]{2,1,0:T(8,128)(2,1)S(1)}, u32[]{:S(2)}, u32[]{:S(2)}) async-start(bf16[8,48,384]{2,1,0:T(8,128)(2,1)} %get-tuple-element.14), calls=%async_computation | async-start | bytes 589824 | tf_op jit(solution)/shard_map/all_to_all | solution.py:94
  16.0 60.4 %all-to-all-start.1 = ((bf16[8,48,1024]{2,1,0:T(8,128)(2,1)}), bf16[8,48,1024]{2,1,0:T(8,128)(2,1)S(1)}, u32[]{:S(2)}, u32[]{:S(2)}) async-start(bf16[8,48,1024]{2,1,0:T(8,128)(2,1)} %get-tuple-element.17), calls=%async_computation.1 | async-start | bytes 1572864 | tf_op jit(solution)/shard_map/all_to_all | solution.py:94
  27.8 16.0 %collective-permute-start = (bf16[32,1024]{1,0:T(8,128)(2,1)S(1)}, bf16[32,1024]{1,0:T(8,128)(2,1)S(1)}, u32[]{:S(2)}, u32[]{:S(2)}) collective-permute-start(bf16[32,1024]{1,0:T(8,128)(2,1)S(1)} %bitcast.20), channel_id=1, source_target_pairs={{0,4},{4,0},{1,5},{5,1},{2,6},{6,2},{3,7},{7,3},{8,12},{12,8},{9,1... | collective-permute-start | bytes 196616 | tf_op jit(solution)/shard_map/ppermute | solution.py:115
  76.4 3.9 %copy-start.2 = (f32[48,1024]{1,0:T(8,128)S(1)}, f32[48,1024]{1,0:T(8,128)}, u32[]{:S(2)}) copy-start(f32[48,1024]{1,0:T(8,128)} %param.10) | copy-start | bytes 589828
  76.4 25.7 %all-to-all-start.2 = ((bf16[8,48,1024]{2,1,0:T(8,128)(2,1)}), bf16[8,48,1024]{2,1,0:T(8,128)(2,1)S(1)}, u32[]{:S(2)}, u32[]{:S(2)}) async-start(bf16[8,48,1024]{2,1,0:T(8,128)(2,1)} %bitcast.4), calls=%async_computation.2 | async-start | bytes 1572864 | tf_op jit(solution)/shard_map/all_to_all | solution.py:94
  80.1 20.4 %copy-start.1 = (bf16[1,48,8192]{2,1,0:T(8,128)(2,1)S(1)}, bf16[1,48,8192]{2,1,0:T(8,128)(2,1)}, u32[]{:S(2)}) copy-start(bf16[1,48,8192]{2,1,0:T(8,128)(2,1)} %param.9) | copy-start | bytes 2359300
  100.5 1.8 %copy-start.3 = (f32[1,48,1024]{2,1,0:T(8,128)S(1)}, f32[1,48,1024]{2,1,0:T(8,128)}, u32[]{:S(2)}) copy-start(f32[1,48,1024]{2,1,0:T(8,128)} %param.13) | copy-start | bytes 589828
  100.5 1.8 %copy-start.4 = (f32[1,48,1024]{2,1,0:T(8,128)S(1)}, f32[1,48,1024]{2,1,0:T(8,128)}, u32[]{:S(2)}) copy-start(f32[1,48,1024]{2,1,0:T(8,128)} %param.14) | copy-start | bytes 589828

commit v4 on v3

--- a/solution.py
+++ b/solution.py
@@ -8,7 +8,7 @@
 
 REPLICA = ("y_near", "core")
 SHARD = ("z_pair", "z_bit", "y_far", "x")
-GROUP = ("z_bit", "x")
+GROUP = ("x", "z_bit")
 
 
 momentum_keep = 0.9
@@ -57,11 +57,11 @@
                     shift = (place - x) * piece % LANES
                     turned = pltpu.roll(tiles[place], shift, 1) if shift else tiles[place]
                     packed = jnp.where(lane // piece == place, turned, packed)
-                packed_buf[bit * 4 + x, :, block * LANES : (block + 1) * LANES] = packed.astype(jnp.bfloat16)
+                packed_buf[x * 2 + bit, :, block * LANES : (block + 1) * LANES] = packed.astype(jnp.bfloat16)
     copies = start_all([pltpu.make_async_copy(packed_buf, packed_out, out_sems.at[count])])
     for j in range(count):
         rows_in[j].wait()
-        copies += start_all([pltpu.make_async_copy(rows_buf.at[:, columns[j]], pieces_out.at[j], out_sems.at[j])])
+        copies += start_all([pltpu.make_async_copy(rows_buf.at[:, columns[j]], pieces_out.at[j % 2 * (count // 2) + j // 2], out_sems.at[j])])
     for copy in copies:
         copy.wait()
 
@@ -118,7 +118,7 @@
     anchor_part = lax.dynamic_slice_in_dim(anchor, offset, part, 1)
     pieces, own_tokens, anchor_part = lax.optimization_barrier((pieces, own_tokens, anchor_part))
 
-    pieces = exchange(pieces, REPLICA)
+    pieces = exchange(pieces, REPLICA[::-1])
 
     both = jnp.where(
         lax.axis_index("y_far") == 0,
@@ -137,14 +137,15 @@
     moved = anchor_part - outer_rate * (outer_grad + momentum_keep * new_velocity)
     moved = lax.all_gather(moved.astype(jnp.bfloat16), REPLICA, axis=1, tiled=True)
 
-    new_anchor = moved.astype(jnp.float32)
-    merged_rows = (blend_keep * rows.astype(jnp.float32) + (1.0 - blend_keep) * new_anchor).astype(jnp.bfloat16)
-
     gradient = jnp.sum(parts.astype(jnp.float32), axis=0)[None]
     new_first = decay_first * first_moment + (1.0 - decay_first) * gradient
     new_second = decay_second * second_moment + (1.0 - decay_second) * gradient * gradient
     stepped = new_first / first_fix / (jnp.sqrt(new_second / second_fix) + epsilon)
     new_weight = inner_weight - inner_rate * (stepped + weight_decay * inner_weight)
+
+    moved, new_weight, new_first, new_second = lax.optimization_barrier((moved, new_weight, new_first, new_second))
+    new_anchor = moved.astype(jnp.float32)
+    merged_rows = (blend_keep * rows.astype(jnp.float32) + (1.0 - blend_keep) * new_anchor).astype(jnp.bfloat16)
     return (new_anchor, merged_rows[None], new_velocity, new_weight, new_first, new_second)
 
 

time: 105 us -> 105 us (level)
    all_gather x1, blocking collectives: 19.5 us -> 21.2 us  [local(): lax.all_gather(moved.astype(jnp.bfloat16), REPLICA, axis=1, tiled=True)]
  transfers between devices with their start and end apart: 4 -> 4, of which waited for: 2 -> 2; matrix products, arithmetic and copies ran while one was open for 4% -> 2% of each run, Pallas kernels for 0% -> 0%
where the time goes in v4:
time: 105 us
  blocking collectives  51.4 us (49%)
  starting transfers between devices  24.1 us (23%)
  waiting for transfers between devices  20.2 us (19%)
  other arithmetic  4.57 us (4%)
  Pallas kernels  2.5 us (2%)
  matrix products  1.46 us (1%)
    all_gather x1, blocking collectives, local(): own_cotangent = lax.all_gather(both, 'z_pair', axis=0, tiled=True)  30.2 us
    all_to_all x3, starting transfers between devices, exchange(): return lax.all_to_all(x, axes, 0, 0, tiled=True)  22.2 us
    all_gather x1, blocking collectives, local(): lax.all_gather(moved.astype(jnp.bfloat16), REPLICA, axis=1, tiled=True)  21.2 us
    ppermute x1, waiting for transfers between devices, local(): other = lax.ppermute(mine, 'y_far', [(0, 1), (1, 0)])  14 us
    all_to_all x3, waiting for transfers between devices, exchange(): return lax.all_to_all(x, axes, 0, 0, tiled=True)  6.28 us
    pallas_call x1, Pallas kernels, prepare(): pl.pallas_call(prepare_kernel, in_specs=[far] * 2, out_specs=[far] * 2, o...  2.5 us
  transfers between devices with their start and end apart: 4, of which 2 were waited for; matrix products, arithmetic and copies ran while one was open for 2% of the time, Pallas kernels for 0%

profile of v4, /device:TPU:1, one launch (start us, length us, event | category | flops | bytes accessed | tf_op | source)
XLA Modules:
  0.0 105.0 jit_solution(3963526713095456114)
XLA Ops:
  0.6 0.0 copy-start
  0.6 0.0 copy-start.5
  0.7 2.5 %prepare.1 = (bf16[8,48,384]{2,1,0:T(8,128)(2,1)}, bf16[8,48,1024]{2,1,0:T(8,128)(2,1)}) custom-call(bf16[48,3072]{1,0:T(8,128)(2,1)} %bitcast.19, bf16[48,8192]{1,0:T(8,128)(2,1)} %bitcast.17), custom_call_target="tpu_custom_call" | custom-call | tf_op jit(solution)/shard_map/prepare/pallas_call | solution.py:74
  3.2 6.7 %all-to-all-start = ((bf16[8,48,384]{2,1,0:T(8,128)(2,1)}), bf16[8,48,384]{2,1,0:T(8,128)(2,1)S(1)}, u32[]{:S(2)}, u32[]{:S(2)}) async-start(bf16[8,48,384]{2,1,0:T(8,128)(2,1)} %get-tuple-element.18), calls=%async_computation | async-start | bytes 589824 | tf_op jit(solution)/shard_map/all_to_all | solution.py:94
  9.8 0.0 copy-done
  9.9 6.3 %all-to-all-done = bf16[8,48,384]{2,1,0:T(8,128)(2,1)S(1)} async-done(((bf16[8,48,384]{2,1,0:T(8,128)(2,1)}), bf16[8,48,384]{2,1,0:T(8,128)(2,1)S(1)}, u32[]{:S(2)}, u32[]{:S(2)}) %all-to-all-start) | async-done | bytes 294944 | tf_op jit(solution)/shard_map/all_to_all | solution.py:94
  16.1 11.8 %all-to-all-start.1 = ((bf16[8,48,1024]{2,1,0:T(8,128)(2,1)}), bf16[8,48,1024]{2,1,0:T(8,128)(2,1)S(1)}, u32[]{:S(2)}, u32[]{:S(2)}) async-start(bf16[8,48,1024]{2,1,0:T(8,128)(2,1)} %get-tuple-element.21), calls=%async_computation.1 | async-start | bytes 1572864 | tf_op jit(solution)/shard_map/all_to_all | solution.py:94
  28.0 0.0 copy-done.5
  28.0 1.9 %collective-permute-start = (bf16[32,1024]{1,0:T(8,128)(2,1)S(1)}, bf16[32,1024]{1,0:T(8,128)(2,1)S(1)}, u32[]{:S(2)}, u32[]{:S(2)}) collective-permute-start(bf16[32,1024]{1,0:T(8,128)(2,1)S(1)} %bitcast.20), channel_id=1, source_target_pairs={{0,4},{4,0},{1,5},{5,1},{2,6},{6,2},{3,7},{7,3},{8,12},{12,8},{9,1... | collective-permute-start | bytes 196616 | tf_op jit(solution)/shard_map/ppermute | solution.py:115
  29.9 14.0 %collective-permute-done = bf16[32,1024]{1,0:T(8,128)(2,1)S(1)} collective-permute-done((bf16[32,1024]{1,0:T(8,128)(2,1)S(1)}, bf16[32,1024]{1,0:T(8,128)(2,1)S(1)}, u32[]{:S(2)}, u32[]{:S(2)}) %collective-permute-start) | collective-permute-done | bytes 65568 | tf_op jit(solution)/shard_map/ppermute | solution.py:115
  43.9 30.2 %all_gather.6 = bf16[384,1024]{1,0:T(8,128)(2,1)S(1)} all-gather(bf16[64,1024]{1,0:T(8,128)(2,1)S(1)} %maximum_select_fusion), channel_id=1, replica_groups=mesh['y_near'=4,'core'=2,'z_pair'=6,'z_bit'=2,'y_far'=2,'x'=4] {'z_pair'}, dimensions={0}, use_global_device_ids=true | all-gather | bytes 917504 | tf_op jit(solution)/shard_map/all_gather | solution.py:128
  74.0 1.5 %convolution_convert_fusion = bf16[384,1024]{1,0:T(8,128)(2,1)} fusion(bf16[384,384]{1,0:T(8,128)(2,1)S(1)} %bitcast.18, bf16[384,1024]{1,0:T(8,128)(2,1)S(1)} %all_gather.6), kind=kOutput, calls=%fused_computation.3 | convolution fusion | flops 302383104 | bytes 1867776 | tf_op jit(solution)/shard_map/dot_general | solution.py:130
  75.5 0.0 copy-start.2
  75.5 0.0 all-to-all-done.1
  75.5 3.7 %all-to-all-start.2 = ((bf16[8,48,1024]{2,1,0:T(8,128)(2,1)}), bf16[8,48,1024]{2,1,0:T(8,128)(2,1)S(1)}, u32[]{:S(2)}, u32[]{:S(2)}) async-start(bf16[8,48,1024]{2,1,0:T(8,128)(2,1)} %bitcast.4), calls=%async_computation.2 | async-start | bytes 1572864 | tf_op jit(solution)/shard_map/all_to_all | solution.py:94
  79.2 0.2 subtract_reduce_fusion
  79.3 0.0 copy-done.2
  79.4 0.7 subtract_convert_fusion
  80.1 0.0 copy-start.3
  80.1 0.0 copy-start.4
  80.1 21.2 %all_gather.7 = bf16[48,8192]{1,0:T(8,128)(2,1)S(1)} all-gather(bf16[48,1024]{1,0:T(8,128)(2,1)S(1)} %get-tuple-element.33), channel_id=1, replica_groups=mesh['y_near'=4,'core'=2,'z_pair'=6,'z_bit'=2,'y_far'=2,'x'=4] {'y_near'..., dimensions={1}, use_global_device_ids=true | all-gather | bytes 884736 | tf_op jit(solution)/shard_map/all_gather | solution.py:138
  101.3 0.0 all-to-all-done.2
  101.3 0.0 copy-start.1
  101.3 0.1 convert_reduce_fusion
  101.5 0.0 copy-done.3
  101.5 0.0 copy-done.4
  101.5 1.9 %multiply_subtract_fusion = (f32[1,48,1024]{2,1,0:T(8,128)}, f32[1,48,1024]{2,1,0:T(8,128)}, f32[1,48,1024]{2,1,0:T(8,128)}) fusion(f32[1,48,1024]{2,1,0:T(8,128)S(1)} %copy-done.3, f32[48,1024]{1,0:T(8,128)S(1)} %convert_reduce_fusion, f32[1,48,1024]{2,1,0:T(8,128)S(1)} %copy-done.4, f32[1,48,1024]{2,1,0:T(8,128)} %param.15), kind=kLoop, calls=%fused_computation.9 | loop fusion | flops 737280 | bytes 1376256 | tf_op jit(solution)/shard_map/sub | solution.py:144
  103.4 0.0 copy-done.1
  103.4 1.7 %fusion = (bf16[1,48,8192]{2,1,0:T(8,128)(2,1)}, f32[48,8192]{1,0:T(8,128)}) fusion(bf16[1,48,8192]{2,1,0:T(8,128)(2,1)S(1)} %copy-done.1, bf16[48,8192]{1,0:T(8,128)(2,1)S(1)} %all_gather.7), kind=kLoop, calls=%fused_computation.4 | loop fusion | flops 1966080 | bytes 3932160 | tf_op jit(solution)/shard_map/broadcast_in_dim | solution.py:149
  (2 shorter events, 0.0 us)
Async XLA Ops:
  0.6 9.2 %copy-start = (f32[48,8192]{1,0:T(8,128)S(1)}, f32[48,8192]{1,0:T(8,128)}, u32[]{:S(2)}) copy-start(f32[48,8192]{1,0:T(8,128)} %param.8) | copy-start | bytes 4718596
  0.6 27.3 %copy-start.5 = (bf16[1,32,1024]{2,1,0:T(8,128)(2,1)S(1)}, bf16[1,32,1024]{2,1,0:T(8,128)(2,1)}, u32[]{:S(2)}) copy-start(bf16[1,32,1024]{2,1,0:T(8,128)(2,1)} %param.12) | copy-start | bytes 196612
  3.2 13.0 %all-to-all-start = ((bf16[8,48,384]{2,1,0:T(8,128)(2,1)}), bf16[8,48,384]{2,1,0:T(8,128)(2,1)S(1)}, u32[]{:S(2)}, u32[]{:S(2)}) async-start(bf16[8,48,384]{2,1,0:T(8,128)(2,1)} %get-tuple-element.18), calls=%async_computation | async-start | bytes 589824 | tf_op jit(solution)/shard_map/all_to_all | solution.py:94
  16.1 59.4 %all-to-all-start.1 = ((bf16[8,48,1024]{2,1,0:T(8,128)(2,1)}), bf16[8,48,1024]{2,1,0:T(8,128)(2,1)S(1)}, u32[]{:S(2)}, u32[]{:S(2)}) async-start(bf16[8,48,1024]{2,1,0:T(8,128)(2,1)} %get-tuple-element.21), calls=%async_computation.1 | async-start | bytes 1572864 | tf_op jit(solution)/shard_map/all_to_all | solution.py:94
  28.0 15.9 %collective-permute-start = (bf16[32,1024]{1,0:T(8,128)(2,1)S(1)}, bf16[32,1024]{1,0:T(8,128)(2,1)S(1)}, u32[]{:S(2)}, u32[]{:S(2)}) collective-permute-start(bf16[32,1024]{1,0:T(8,128)(2,1)S(1)} %bitcast.20), channel_id=1, source_target_pairs={{0,4},{4,0},{1,5},{5,1},{2,6},{6,2},{3,7},{7,3},{8,12},{12,8},{9,1... | collective-permute-start | bytes 196616 | tf_op jit(solution)/shard_map/ppermute | solution.py:115
  75.5 3.9 %copy-start.2 = (f32[48,1024]{1,0:T(8,128)S(1)}, f32[48,1024]{1,0:T(8,128)}, u32[]{:S(2)}) copy-start(f32[48,1024]{1,0:T(8,128)} %param.10) | copy-start | bytes 589828
  75.5 25.8 %all-to-all-start.2 = ((bf16[8,48,1024]{2,1,0:T(8,128)(2,1)}), bf16[8,48,1024]{2,1,0:T(8,128)(2,1)S(1)}, u32[]{:S(2)}, u32[]{:S(2)}) async-start(bf16[8,48,1024]{2,1,0:T(8,128)(2,1)} %bitcast.4), calls=%async_computation.2 | async-start | bytes 1572864 | tf_op jit(solution)/shard_map/all_to_all | solution.py:94
  80.1 21.4 %copy-start.3 = (f32[1,48,1024]{2,1,0:T(8,128)S(1)}, f32[1,48,1024]{2,1,0:T(8,128)}, u32[]{:S(2)}) copy-start(f32[1,48,1024]{2,1,0:T(8,128)} %param.13) | copy-start | bytes 589828
  80.1 21.4 %copy-start.4 = (f32[1,48,1024]{2,1,0:T(8,128)S(1)}, f32[1,48,1024]{2,1,0:T(8,128)}, u32[]{:S(2)}) copy-start(f32[1,48,1024]{2,1,0:T(8,128)} %param.14) | copy-start | bytes 589828
  101.3 2.0 %copy-start.1 = (bf16[1,48,8192]{2,1,0:T(8,128)(2,1)S(1)}, bf16[1,48,8192]{2,1,0:T(8,128)(2,1)}, u32[]{:S(2)}) copy-start(bf16[1,48,8192]{2,1,0:T(8,128)(2,1)} %param.9) | copy-start | bytes 2359300

commit v5 on v4

--- a/solution.py
+++ b/solution.py
@@ -36,16 +36,23 @@
 ):
     height, tokens = features_ref.shape
     count, _, part = pieces_out.shape
-    features_in = pltpu.make_async_copy(features_ref, features_buf, in_sems.at[count])
-    features_in.start()
+    blocks = tokens // (8 * LANES)
+    wide = [pl.ds(block * 8 * LANES, 8 * LANES) for block in range(blocks)]
+    features_in = start_all(
+        [
+            pltpu.make_async_copy(features_ref.at[:, wide[k]], features_buf.at[:, wide[k]], in_sems.at[count + k])
+            for k in range(blocks)
+        ]
+    )
     columns = [pl.ds(j * part, part) for j in range(count)]
     rows_in = start_all(
         [pltpu.make_async_copy(rows_ref.at[:, columns[j]], rows_buf.at[:, columns[j]], in_sems.at[j]) for j in range(count)]
     )
     piece = LANES // 4
     lane = lax.broadcasted_iota(jnp.int32, (height, LANES), 1)
-    features_in.wait()
-    for block in range(tokens // (8 * LANES)):
+    copies = []
+    for block in range(blocks):
+        features_in[block].wait()
         for bit in range(2):
             tiles = []
             for place in range(4):
@@ -58,7 +65,10 @@
                     turned = pltpu.roll(tiles[place], shift, 1) if shift else tiles[place]
                     packed = jnp.where(lane // piece == place, turned, packed)
                 packed_buf[x * 2 + bit, :, block * LANES : (block + 1) * LANES] = packed.astype(jnp.bfloat16)
-    copies = start_all([pltpu.make_async_copy(packed_buf, packed_out, out_sems.at[count])])
+        lanes = pl.ds(block * LANES, LANES)
+        copies += start_all(
+            [pltpu.make_async_copy(packed_buf.at[:, :, lanes], packed_out.at[:, :, lanes], out_sems.at[count + block])]
+        )
     for j in range(count):
         rows_in[j].wait()
         copies += start_all([pltpu.make_async_copy(rows_buf.at[:, columns[j]], pieces_out.at[j % 2 * (count // 2) + j // 2], out_sems.at[j])])
@@ -83,8 +93,8 @@
             pltpu.VMEM(features.shape, features.dtype),
             pltpu.VMEM(rows.shape, rows.dtype),
             pltpu.VMEM((8, height, tokens // 8), jnp.bfloat16),
-            pltpu.SemaphoreType.DMA((count + 1,)),
-            pltpu.SemaphoreType.DMA((count + 1,)),
+            pltpu.SemaphoreType.DMA((count + tokens // (8 * LANES),)),
+            pltpu.SemaphoreType.DMA((count + tokens // (8 * LANES),)),
         ],
         name="prepare",
     )(features, rows)
@@ -137,15 +147,14 @@
     moved = anchor_part - outer_rate * (outer_grad + momentum_keep * new_velocity)
     moved = lax.all_gather(moved.astype(jnp.bfloat16), REPLICA, axis=1, tiled=True)
 
+    new_anchor = moved.astype(jnp.float32)
+    merged_rows = (blend_keep * rows.astype(jnp.float32) + (1.0 - blend_keep) * new_anchor).astype(jnp.bfloat16)
+
     gradient = jnp.sum(parts.astype(jnp.float32), axis=0)[None]
     new_first = decay_first * first_moment + (1.0 - decay_first) * gradient
     new_second = decay_second * second_moment + (1.0 - decay_second) * gradient * gradient
     stepped = new_first / first_fix / (jnp.sqrt(new_second / second_fix) + epsilon)
     new_weight = inner_weight - inner_rate * (stepped + weight_decay * inner_weight)
-
-    moved, new_weight, new_first, new_second = lax.optimization_barrier((moved, new_weight, new_first, new_second))
-    new_anchor = moved.astype(jnp.float32)
-    merged_rows = (blend_keep * rows.astype(jnp.float32) + (1.0 - blend_keep) * new_anchor).astype(jnp.bfloat16)
     return (new_anchor, merged_rows[None], new_velocity, new_weight, new_first, new_second)
 
 

time: 105 us -> 105 us (level)
  transfers between devices with their start and end apart: 4 -> 4, of which waited for: 2 -> 2; matrix products, arithmetic and copies ran while one was open for 2% -> 4% of each run, Pallas kernels for 0% -> 0%
where the time goes in v5:
time: 105 us
  blocking collectives  51.3 us (49%)
  starting transfers between devices  24.1 us (23%)
  waiting for transfers between devices  20.2 us (19%)
  other arithmetic  4.5 us (4%)
  Pallas kernels  2.56 us (2%)
  matrix products  1.47 us (1%)
    all_gather x1, blocking collectives, local(): own_cotangent = lax.all_gather(both, 'z_pair', axis=0, tiled=True)  30.2 us
    all_to_all x3, starting transfers between devices, exchange(): return lax.all_to_all(x, axes, 0, 0, tiled=True)  22.2 us
    all_gather x1, blocking collectives, local(): lax.all_gather(moved.astype(jnp.bfloat16), REPLICA, axis=1, tiled=True)  21.1 us
    ppermute x1, waiting for transfers between devices, local(): other = lax.ppermute(mine, 'y_far', [(0, 1), (1, 0)])  14 us
    all_to_all x3, waiting for transfers between devices, exchange(): return lax.all_to_all(x, axes, 0, 0, tiled=True)  6.28 us
    pallas_call x1, Pallas kernels, prepare(): pl.pallas_call(prepare_kernel, in_specs=[far] * 2, out_specs=[far] * 2, o...  2.56 us
  transfers between devices with their start and end apart: 4, of which 2 were waited for; matrix products, arithmetic and copies ran while one was open for 4% of the time, Pallas kernels for 0%

profile of v5, /device:TPU:1, one launch (start us, length us, event | category | flops | bytes accessed | tf_op | source)
XLA Modules:
  0.0 104.9 jit_solution(2590896521457037518)
XLA Ops:
  0.6 0.0 copy-start
  0.6 0.0 copy-start.5
  0.7 2.6 %prepare.1 = (bf16[8,48,384]{2,1,0:T(8,128)(2,1)}, bf16[8,48,1024]{2,1,0:T(8,128)(2,1)}) custom-call(bf16[48,3072]{1,0:T(8,128)(2,1)} %bitcast.19, bf16[48,8192]{1,0:T(8,128)(2,1)} %bitcast.17), custom_call_target="tpu_custom_call" | custom-call | tf_op jit(solution)/shard_map/prepare/pallas_call | solution.py:84
  3.2 6.7 %all-to-all-start = ((bf16[8,48,384]{2,1,0:T(8,128)(2,1)}), bf16[8,48,384]{2,1,0:T(8,128)(2,1)S(1)}, u32[]{:S(2)}, u32[]{:S(2)}) async-start(bf16[8,48,384]{2,1,0:T(8,128)(2,1)} %get-tuple-element.14), calls=%async_computation | async-start | bytes 589824 | tf_op jit(solution)/shard_map/all_to_all | solution.py:104
  9.9 0.0 copy-done
  9.9 6.3 %all-to-all-done = bf16[8,48,384]{2,1,0:T(8,128)(2,1)S(1)} async-done(((bf16[8,48,384]{2,1,0:T(8,128)(2,1)}), bf16[8,48,384]{2,1,0:T(8,128)(2,1)S(1)}, u32[]{:S(2)}, u32[]{:S(2)}) %all-to-all-start) | async-done | bytes 294944 | tf_op jit(solution)/shard_map/all_to_all | solution.py:104
  16.2 11.8 %all-to-all-start.1 = ((bf16[8,48,1024]{2,1,0:T(8,128)(2,1)}), bf16[8,48,1024]{2,1,0:T(8,128)(2,1)S(1)}, u32[]{:S(2)}, u32[]{:S(2)}) async-start(bf16[8,48,1024]{2,1,0:T(8,128)(2,1)} %get-tuple-element.17), calls=%async_computation.1 | async-start | bytes 1572864 | tf_op jit(solution)/shard_map/all_to_all | solution.py:104
  28.0 0.0 copy-done.5
  28.0 1.9 %collective-permute-start = (bf16[32,1024]{1,0:T(8,128)(2,1)S(1)}, bf16[32,1024]{1,0:T(8,128)(2,1)S(1)}, u32[]{:S(2)}, u32[]{:S(2)}) collective-permute-start(bf16[32,1024]{1,0:T(8,128)(2,1)S(1)} %bitcast.20), channel_id=1, source_target_pairs={{0,4},{4,0},{1,5},{5,1},{2,6},{6,2},{3,7},{7,3},{8,12},{12,8},{9,1... | collective-permute-start | bytes 196616 | tf_op jit(solution)/shard_map/ppermute | solution.py:125
  29.9 14.0 %collective-permute-done = bf16[32,1024]{1,0:T(8,128)(2,1)S(1)} collective-permute-done((bf16[32,1024]{1,0:T(8,128)(2,1)S(1)}, bf16[32,1024]{1,0:T(8,128)(2,1)S(1)}, u32[]{:S(2)}, u32[]{:S(2)}) %collective-permute-start) | collective-permute-done | bytes 65568 | tf_op jit(solution)/shard_map/ppermute | solution.py:125
  43.9 30.2 %all_gather.6 = bf16[384,1024]{1,0:T(8,128)(2,1)S(1)} all-gather(bf16[64,1024]{1,0:T(8,128)(2,1)S(1)} %maximum_select_fusion), channel_id=1, replica_groups=mesh['y_near'=4,'core'=2,'z_pair'=6,'z_bit'=2,'y_far'=2,'x'=4] {'z_pair'}, dimensions={0}, use_global_device_ids=true | all-gather | bytes 917504 | tf_op jit(solution)/shard_map/all_gather | solution.py:138
  74.1 1.5 %convolution_convert_fusion = bf16[384,1024]{1,0:T(8,128)(2,1)} fusion(bf16[384,384]{1,0:T(8,128)(2,1)S(1)} %bitcast.18, bf16[384,1024]{1,0:T(8,128)(2,1)S(1)} %all_gather.6), kind=kOutput, calls=%fused_computation.3 | convolution fusion | flops 302383104 | bytes 1867776 | tf_op jit(solution)/shard_map/dot_general | solution.py:140
  75.5 0.0 copy-start.2
  75.5 0.0 all-to-all-done.1
  75.5 3.7 %all-to-all-start.2 = ((bf16[8,48,1024]{2,1,0:T(8,128)(2,1)}), bf16[8,48,1024]{2,1,0:T(8,128)(2,1)S(1)}, u32[]{:S(2)}, u32[]{:S(2)}) async-start(bf16[8,48,1024]{2,1,0:T(8,128)(2,1)} %bitcast.4), calls=%async_computation.2 | async-start | bytes 1572864 | tf_op jit(solution)/shard_map/all_to_all | solution.py:104
  79.2 0.0 copy-start.1
  79.2 0.2 subtract_reduce_fusion
  79.4 0.0 copy-done.2
  79.4 0.7 subtract_convert_fusion
  80.2 21.1 %all_gather.7 = bf16[48,8192]{1,0:T(8,128)(2,1)S(1)} all-gather(bf16[48,1024]{1,0:T(8,128)(2,1)S(1)} %get-tuple-element.25), channel_id=1, replica_groups=mesh['y_near'=4,'core'=2,'z_pair'=6,'z_bit'=2,'y_far'=2,'x'=4] {'y_near'..., dimensions={1}, use_global_device_ids=true | all-gather | bytes 884736 | tf_op jit(solution)/shard_map/all_gather | solution.py:148
  101.3 0.0 copy-done.1
  101.3 0.0 copy-start.3
  101.3 0.0 copy-start.4
  101.3 1.7 %fusion = (bf16[1,48,8192]{2,1,0:T(8,128)(2,1)}, f32[48,8192]{1,0:T(8,128)}) fusion(bf16[1,48,8192]{2,1,0:T(8,128)(2,1)S(1)} %copy-done.1, bf16[48,8192]{1,0:T(8,128)(2,1)S(1)} %all_gather.7), kind=kLoop, calls=%fused_computation.4 | loop fusion | flops 1966080 | bytes 3932160 | tf_op jit(solution)/shard_map/broadcast_in_dim | solution.py:158
  102.9 0.0 all-to-all-done.2
  102.9 0.1 convert_reduce_fusion
  103.0 0.0 copy-done.3
  103.1 0.0 copy-done.4
  103.1 1.8 %multiply_subtract_fusion = (f32[1,48,1024]{2,1,0:T(8,128)}, f32[1,48,1024]{2,1,0:T(8,128)}, f32[1,48,1024]{2,1,0:T(8,128)}) fusion(f32[1,48,1024]{2,1,0:T(8,128)S(1)} %copy-done.3, f32[48,1024]{1,0:T(8,128)S(1)} %convert_reduce_fusion, f32[1,48,1024]{2,1,0:T(8,128)S(1)} %copy-done.4, f32[1,48,1024]{2,1,0:T(8,128)} %param.15), kind=kLoop, calls=%fused_computation.9 | loop fusion | flops 737280 | bytes 1376256 | tf_op jit(solution)/shard_map/sub | solution.py:157
  (2 shorter events, 0.0 us)
Async XLA Ops:
  0.6 9.2 %copy-start = (f32[48,8192]{1,0:T(8,128)S(1)}, f32[48,8192]{1,0:T(8,128)}, u32[]{:S(2)}) copy-start(f32[48,8192]{1,0:T(8,128)} %param.8) | copy-start | bytes 4718596
  0.6 27.4 %copy-start.5 = (bf16[1,32,1024]{2,1,0:T(8,128)(2,1)S(1)}, bf16[1,32,1024]{2,1,0:T(8,128)(2,1)}, u32[]{:S(2)}) copy-start(bf16[1,32,1024]{2,1,0:T(8,128)(2,1)} %param.12) | copy-start | bytes 196612
  3.2 13.0 %all-to-all-start = ((bf16[8,48,384]{2,1,0:T(8,128)(2,1)}), bf16[8,48,384]{2,1,0:T(8,128)(2,1)S(1)}, u32[]{:S(2)}, u32[]{:S(2)}) async-start(bf16[8,48,384]{2,1,0:T(8,128)(2,1)} %get-tuple-element.14), calls=%async_computation | async-start | bytes 589824 | tf_op jit(solution)/shard_map/all_to_all | solution.py:104
  16.2 59.4 %all-to-all-start.1 = ((bf16[8,48,1024]{2,1,0:T(8,128)(2,1)}), bf16[8,48,1024]{2,1,0:T(8,128)(2,1)S(1)}, u32[]{:S(2)}, u32[]{:S(2)}) async-start(bf16[8,48,1024]{2,1,0:T(8,128)(2,1)} %get-tuple-element.17), calls=%async_computation.1 | async-start | bytes 1572864 | tf_op jit(solution)/shard_map/all_to_all | solution.py:104
  28.0 15.9 %collective-permute-start = (bf16[32,1024]{1,0:T(8,128)(2,1)S(1)}, bf16[32,1024]{1,0:T(8,128)(2,1)S(1)}, u32[]{:S(2)}, u32[]{:S(2)}) collective-permute-start(bf16[32,1024]{1,0:T(8,128)(2,1)S(1)} %bitcast.20), channel_id=1, source_target_pairs={{0,4},{4,0},{1,5},{5,1},{2,6},{6,2},{3,7},{7,3},{8,12},{12,8},{9,1... | collective-permute-start | bytes 196616 | tf_op jit(solution)/shard_map/ppermute | solution.py:125
  75.5 3.9 %copy-start.2 = (f32[48,1024]{1,0:T(8,128)S(1)}, f32[48,1024]{1,0:T(8,128)}, u32[]{:S(2)}) copy-start(f32[48,1024]{1,0:T(8,128)} %param.10) | copy-start | bytes 589828
  75.5 27.4 %all-to-all-start.2 = ((bf16[8,48,1024]{2,1,0:T(8,128)(2,1)}), bf16[8,48,1024]{2,1,0:T(8,128)(2,1)S(1)}, u32[]{:S(2)}, u32[]{:S(2)}) async-start(bf16[8,48,1024]{2,1,0:T(8,128)(2,1)} %bitcast.4), calls=%async_computation.2 | async-start | bytes 1572864 | tf_op jit(solution)/shard_map/all_to_all | solution.py:104
  79.2 22.0 %copy-start.1 = (bf16[1,48,8192]{2,1,0:T(8,128)(2,1)S(1)}, bf16[1,48,8192]{2,1,0:T(8,128)(2,1)}, u32[]{:S(2)}) copy-start(bf16[1,48,8192]{2,1,0:T(8,128)(2,1)} %param.9) | copy-start | bytes 2359300
  101.3 1.8 %copy-start.3 = (f32[1,48,1024]{2,1,0:T(8,128)S(1)}, f32[1,48,1024]{2,1,0:T(8,128)}, u32[]{:S(2)}) copy-start(f32[1,48,1024]{2,1,0:T(8,128)} %param.13) | copy-start | bytes 589828
  101.3 1.8 %copy-start.4 = (f32[1,48,1024]{2,1,0:T(8,128)S(1)}, f32[1,48,1024]{2,1,0:T(8,128)}, u32[]{:S(2)}) copy-start(f32[1,48,1024]{2,1,0:T(8,128)} %param.14) | copy-start | bytes 589828
